TPU v7x, 32 devices: a whole 2x2x4 slice. The times are simulated.
32 devices in a mesh: seq: 8 (over z, core), vocab: 4 (over y, x).
Axes of the slice: x: 2, y: 2, z: 4, core: 2. Of those that a mesh axis runs over, the one named last changes fastest.
Arguments:
- token_ids: int32 [1024], P('seq'), may hold values from 0 to 76031, as said below
- routes: int32 [256, 1], P('seq'), may hold values from 0 to 7; in each aligned block of 32 rows (0 to 31, 32 to 63, ...) at most 8 rows name the same one
- splice_start: int32 [8], P('seq'), may hold values from 0 to 64
- vision: bfloat16 [256, 5120], P('seq'), may hold values from -6 to 6
- ln_gain: float32 [1280], replicated, may hold values from 0.25 to 1.75
- table: bfloat16 [76032, 8192], P('seq', 'vocab'), may hold values from -6 to 6
- w_fc1: bfloat16 [5120, 5120], P('seq', 'vocab'), may hold values from -0.078125 to 0.078125
- w_fc2: bfloat16 [5120, 8192], P('seq', 'vocab'), may hold values from -0.078125 to 0.078125
Outputs:
- embedded: bfloat16 [1024, 8192], P('seq', 'vocab')
Inputs may be any that keep to these rules, and one draw needn't show every extreme that they name: `routes`: among the rows of one shard of 32 rows no sequence is named by more than 8 rows. `token_ids`: split the vocabulary into 8 equal ranges of consecutive ids; within one sequence of 128 tokens at most 32 ids fall in one range, and every sequence has a range with exactly 32.
All inputs are finite; a program needn't handle non-finite values.
Results may differ from a plain program's by a relative error of at most 0.0055.
Values may be sent and summed in bfloat16 or wider, within the bound.
A program may use at most 128 MiB of HBM per device.

v0:
```python
import math

import jax
import jax.numpy as jnp
from jax import lax
from jax.experimental import pallas as pl
from jax.experimental.pallas import tpu as pltpu
from jax.sharding import PartitionSpec as P


TILE = 8


def gather_kernel(ids_ref, pick_ref, table_ref, out_ref, held, sems):
    groups, cap, _ = out_ref.shape

    def issue(g, carry):
        def one(k, c):
            row = pl.multiple_of(ids_ref[g, k] // TILE * TILE, TILE)
            at = pl.multiple_of((g * cap + k) * TILE, TILE)
            pltpu.make_async_copy(
                table_ref.at[pl.ds(row, TILE), :], held.at[pl.ds(at, TILE), :], sems.at[g]
            ).start()
            return c

        return lax.fori_loop(0, cap, one, carry)

    lax.fori_loop(0, groups, issue, 0)

    def finish(g, carry):
        at = pl.multiple_of(g * cap * TILE, TILE)
        block = held.at[pl.ds(at, cap * TILE), :]
        pltpu.make_async_copy(block, block, sems.at[g]).wait()
        out_ref[g] = jnp.dot(
            pick_ref[g], block[...], preferred_element_type=jnp.float32
        ).astype(out_ref.dtype)
        return carry

    lax.fori_loop(0, groups, finish, 0)


def gather_rows(local_ids, table):
    groups, cap = local_ids.shape
    width = table.shape[1]
    lane = jnp.arange(cap * TILE, dtype=jnp.int32)
    slot = jnp.arange(cap, dtype=jnp.int32)[None, :] * TILE + local_ids % TILE
    pick = (slot[:, :, None] == lane[None, None, :]).astype(jnp.bfloat16)
    return pl.pallas_call(
        gather_kernel,
        out_shape=jax.ShapeDtypeStruct((groups, cap, width), table.dtype),
        in_specs=[
            pl.BlockSpec(memory_space=pltpu.SMEM),
            pl.BlockSpec(memory_space=pltpu.VMEM),
            pl.BlockSpec(memory_space=pl.ANY),
        ],
        out_specs=pl.BlockSpec(memory_space=pltpu.VMEM),
        scratch_shapes=[
            pltpu.VMEM((groups * cap * TILE, width), table.dtype),
            pltpu.SemaphoreType.DMA((groups,)),
        ],
        name="gather_rows",
    )(local_ids, pick, table)


def route_plan(token_ids, routes, splice_start, shard_rows):
    seq_count = lax.axis_size("seq")
    seq_index = lax.axis_index("seq")
    local_rows = token_ids.shape[0]
    slot_rows = routes.shape[0]
    pair_cap = 2 * slot_rows // seq_count
    id_cap = 2 * local_rows // seq_count
    both = lax.all_gather(jnp.concatenate([token_ids, routes[:, 0]]), "seq", axis=0)
    all_ids, all_routes = both[:, :local_rows], both[:, local_rows:]
    mine = all_ids // shard_rows == seq_index
    place = jnp.cumsum(mine.astype(jnp.int32), axis=1) - 1
    hit = mine[:, None, :] & (
        place[:, None, :] == jnp.arange(id_cap, dtype=jnp.int32)[None, :, None]
    )
    local_ids = jnp.sum(jnp.where(hit, all_ids[:, None, :] - seq_index * shard_rows, 0), axis=2)
    home = token_ids // shard_rows
    same = (home[None, :] == home[:, None]) & (
        jnp.arange(local_rows)[None, :] < jnp.arange(local_rows)[:, None]
    )
    arrive = home * id_cap + jnp.sum(same.astype(jnp.int32), axis=1)
    own = routes[:, 0]
    earlier = (own[None, :] == own[:, None]) & (
        jnp.arange(slot_rows)[None, :] < jnp.arange(slot_rows)[:, None]
    )
    slot_of = own * pair_cap + jnp.sum(earlier.astype(jnp.int32), axis=1)
    selector = (
        slot_of[None, :] == jnp.arange(seq_count * pair_cap, dtype=jnp.int32)[:, None]
    ).astype(jnp.bfloat16)
    counts = jnp.sum((all_routes == seq_index).astype(jnp.int32), axis=1)
    before = jnp.arange(seq_count)[None, :] < jnp.arange(seq_count)[:, None]
    offset = jnp.sum(jnp.where(before, counts[None, :], 0), axis=1)
    within = jnp.arange(pair_cap, dtype=jnp.int32)
    position = jnp.where(
        within[None, :] < counts[:, None],
        splice_start[0] + offset[:, None] + within[None, :],
        -1,
    ).reshape(-1)
    rows = jnp.arange(local_rows, dtype=jnp.int32)
    image = position[None, :] == rows[:, None]
    first = splice_start[0]
    is_image = (rows >= first) & (rows < first + jnp.sum(counts))
    text = (
        arrive[:, None] == jnp.arange(seq_count * id_cap, dtype=jnp.int32)[None, :]
    ) & ~is_image[:, None]
    return local_ids, selector, image.astype(jnp.bfloat16), text.astype(jnp.bfloat16)


def mega_kernel(
    vision_ref, gain_ref, w1_hbm, w2_hbm, text_ref, selector_ref, image_ref, placed_ref, out_ref,
    w1, w2, x_send, x_recv, half_send, half_recv, half_own, cross_send, cross_recv,
    h_send, h_recv, pair_send, pair_recv, pair_own, part_send, part_recv,
    row_send, row_recv, text_recv, total,
    w_sem, x_sems, half_sems, cross_sems, h_send_sems, h_recv_sems,
    pair_sems, part_sems, row_sems, text_sems,
):
    n, voc = lax.axis_size("seq"), lax.axis_size("vocab")
    s, v = lax.axis_index("seq"), lax.axis_index("vocab")
    chips = n // 2
    z, c = s // 2, s % 2
    split = n // voc
    f32, bf16 = jnp.float32, jnp.bfloat16
    slots = vision_ref.shape[0]

    def at(seq, vocab):
        return dict(device_id=(seq, vocab), device_id_type=pl.DeviceIdType.MESH)

    load1 = pltpu.make_async_copy(w1_hbm, w1, w_sem.at[0])
    load2 = pltpu.make_async_copy(w2_hbm, w2, w_sem.at[1])
    load1.start()
    load2.start()

    feeds = s // split
    barrier = pltpu.get_barrier_semaphore()
    for d in range(1, n):
        pl.semaphore_signal(barrier, inc=1, **at(lax.rem(s + d, n), v))
    for e in range(1, voc):
        for j in range(split):
            pl.semaphore_signal(barrier, inc=1, **at(v * split + j, lax.rem(v + e, voc)))

    @pl.when(feeds != v)
    def _():
        for r in range(n):
            pl.semaphore_signal(barrier, inc=1, **at(r, feeds))

    group = gain_ref.shape[1]
    depth = x_send.shape[2]
    for g in range(vision_ref.shape[1] // group):
        values = vision_ref[:, g * group : (g + 1) * group].astype(f32)
        center = values - jnp.mean(values, axis=-1, keepdims=True)
        spread = jnp.mean(center * center, axis=-1, keepdims=True)
        normed = (center / jnp.sqrt(spread + 1e-06) * gain_ref[...]).astype(bf16)
        for k in range(group // depth):
            x_send[g * (group // depth) + k] = normed[:, k * depth : (k + 1) * depth]

    pl.semaphore_wait(barrier, n - 1 + (voc - 1) * split + jnp.where(feeds != v, n, 0))

    def to_peer(source, target, sems, d, seq):
        copy = pltpu.make_async_remote_copy(
            src_ref=source,
            dst_ref=target,
            send_sem=sems.at[0, d],
            recv_sem=sems.at[1, d],
            **at(seq, v),
        )
        copy.start()
        return copy

    copies = []
    for d in range(1, n):
        peer = lax.rem(s + d, n)
        copies.append(to_peer(x_send.at[peer], x_recv.at[c, z], x_sems, d, peer))
    x_recv[c, z] = x_send[s]

    texts = []

    def send_text(ds):
        for d in ds:
            peer = lax.rem(s + d, n)
            texts.append(to_peer(text_ref.at[peer], text_recv.at[s], text_sems, d, peer))

    send_text(TEXT_A(n))
    text_recv[s] = text_ref[s]
    for copy in copies:
        copy.wait()

    def columns(width):
        return 256 if width % 256 == 0 else width

    def summed(lhs_ref, weight, to_sib, from_sib, own, send, recv, sems_pair, sems_part, ds):
        width = weight.shape[1]
        step = columns(width)
        rows = chips * slots
        for core, keep in ((1 - c, False), (c, True)):
            lhs = lhs_ref[core].reshape(rows, weight.shape[0])
            for k in range(0, width, step):
                part = jnp.dot(lhs, weight[:, k : k + step], preferred_element_type=f32)
                if keep:
                    own[:, k : k + step] = part
                else:
                    to_sib[:, k : k + step] = part.astype(bf16)
            if not keep:
                swap = to_peer(to_sib, from_sib, sems_pair, 0, s + 1 - 2 * c)
        swap.wait()
        sent = []
        for d in range(1, chips):
            other = lax.rem(z + d, chips)
            span = pl.ds(pl.multiple_of(other * slots, slots), slots)
            send[d] = (own[span, :] + from_sib[span, :].astype(f32)).astype(bf16)
            sent.append(to_peer(send.at[d], recv.at[d], sems_part, d, other * 2 + c))
        send_text(ds)
        span = pl.ds(pl.multiple_of(z * slots, slots), slots)
        value = own[span, :] + from_sib[span, :].astype(f32)
        for copy in sent:
            copy.wait()
        for d in range(1, chips):
            value = value + recv[d].astype(f32)
        return value

    load1.wait()
    pre = summed(x_recv, w1, half_send, half_recv, half_own, cross_send, cross_recv,
                 half_sems, cross_sems, TEXT_B(n))
    hidden = (0.5 * pre * (1.0 + lax.erf(pre * math.sqrt(0.5)))).astype(bf16)
    inner = h_send.shape[2]
    for j in range(split):
        h_send[j] = hidden[:, j * inner : (j + 1) * inner]

    def hidden_copy(e, j):
        return pltpu.make_async_remote_copy(
            src_ref=h_send.at[j],
            dst_ref=h_recv.at[c, z],
            send_sem=h_send_sems.at[e, j],
            recv_sem=h_recv_sems.at[s],
            **at(v * split + j, lax.rem(v + e, voc)),
        )

    for j in range(split):
        target = v * split + j

        @pl.when(target != s)
        def _():
            hidden_copy(0, j).start()

        @pl.when(target == s)
        def _():
            h_recv[c, z] = h_send[j]

        for e in range(1, voc):
            hidden_copy(e, j).start()
    send_text(TEXT_C(n))
    load2.wait()
    for r in range(n):
        def arrived():
            pltpu.make_async_remote_copy(
                src_ref=h_send.at[0],
                dst_ref=h_recv.at[r % 2, r // 2],
                send_sem=h_send_sems.at[0, 0],
                recv_sem=h_recv_sems.at[r],
                **at(lax.rem(s + 1, n), v),
            ).wait_recv()

        pl.when(jnp.logical_or(r != s, feeds != v))(arrived)

    merged = summed(h_recv, w2, pair_send, pair_recv, pair_own, part_send, part_recv,
                    pair_sems, part_sems, TEXT_D(n)).astype(bf16)

    width = w2.shape[1]
    cap = row_send.shape[1]
    outgoing = jnp.dot(selector_ref[...], merged, preferred_element_type=f32).astype(bf16)
    for t in range(n):
        row_send[t] = outgoing[t * cap : (t + 1) * cap]
    copies = []
    for d in range(1, n):
        peer = lax.rem(s + d, n)
        copies.append(to_peer(row_send.at[peer], row_recv.at[s], row_sems, d, peer))
    row_recv[s] = row_send[s]
    for copy in texts:
        copy.wait()
    step = columns(width)
    found = text_recv[...].reshape(-1, width)
    for k in range(0, width, step):
        total[:, k : k + step] = jnp.dot(
            placed_ref[...], found[:, k : k + step], preferred_element_type=f32
        )
    for copy in copies:
        copy.wait()
    for k in range(0, width, step):
        value = total[:, k : k + step]
        block = row_recv[:, :, k : k + step].astype(f32).reshape(n * cap, step).astype(bf16)
        value = value + jnp.dot(image_ref[...], block, preferred_element_type=f32)
        out_ref[:, k : k + step] = value.astype(bf16)
    for j in range(split):
        for e in range(voc):
            def left():
                hidden_copy(e, j).wait_send()

            if e == 0:
                pl.when(v * split + j != s)(left)
            else:
                left()


def TEXT_A(n):
    return range(1, 2)


def TEXT_B(n):
    return range(2, n // 2)


def TEXT_C(n):
    return range(n // 2, 3 * n // 4)


def TEXT_D(n):
    return range(3 * n // 4, n)


def mega(vision, gain, w1, w2, text, selector, image_pick, text_pick):
    n, voc = lax.axis_size("seq"), lax.axis_size("vocab")
    slots = vision.shape[0]
    rows = n // 2 * slots
    depth, mid = w1.shape
    inner, width = w2.shape
    cap = selector.shape[0] // n
    bf16, f32 = jnp.bfloat16, jnp.float32
    vmem = pl.BlockSpec(memory_space=pltpu.VMEM)
    hbm = pl.BlockSpec(memory_space=pl.ANY)
    dma = pltpu.SemaphoreType.DMA
    return pl.pallas_call(
        mega_kernel,
        out_shape=jax.ShapeDtypeStruct((image_pick.shape[0], width), bf16),
        in_specs=[vmem, vmem, hbm, hbm, vmem, vmem, vmem, vmem],
        out_specs=vmem,
        scratch_shapes=[
            pltpu.VMEM(w1.shape, bf16),
            pltpu.VMEM(w2.shape, bf16),
            pltpu.VMEM((n, slots, depth), bf16),
            pltpu.VMEM((2, n // 2, slots, depth), bf16),
            pltpu.VMEM((rows, mid), bf16),
            pltpu.VMEM((rows, mid), bf16),
            pltpu.VMEM((rows, mid), f32),
            pltpu.VMEM((n // 2, slots, mid), bf16),
            pltpu.VMEM((n // 2, slots, mid), bf16),
            pltpu.VMEM((n // voc, slots, inner), bf16),
            pltpu.VMEM((2, n // 2, slots, inner), bf16),
            pltpu.VMEM((rows, width), bf16),
            pltpu.VMEM((rows, width), bf16),
            pltpu.VMEM((rows, width), f32),
            pltpu.VMEM((n // 2, slots, width), bf16),
            pltpu.VMEM((n // 2, slots, width), bf16),
            pltpu.VMEM((n, cap, width), bf16),
            pltpu.VMEM((n, cap, width), bf16),
            pltpu.VMEM(text.shape, bf16),
            pltpu.VMEM((image_pick.shape[0], width), f32),
            dma((2,)),
            dma((2, n)),
            dma((2, 1)),
            dma((2, n // 2)),
            dma((voc, n // voc)),
            dma((n,)),
            dma((2, 1)),
            dma((2, n // 2)),
            dma((2, n)),
            dma((2, n)),
        ],
        compiler_params=pltpu.CompilerParams(
            collective_id=0, has_side_effects=True, vmem_limit_bytes=40 * 1024 * 1024
        ),
        name="merger",
    )(vision, gain[None, :], w1, w2, text, selector, image_pick, text_pick)


def on_device(token_ids, routes, splice_start, vision, ln_gain, table, w_fc1, w_fc2):
    local_ids, selector, image_pick, text_pick = route_plan(
        token_ids, routes, splice_start, table.shape[0]
    )
    text = gather_rows(local_ids, table)
    return mega(vision, ln_gain, w_fc1, w_fc2, text, selector, image_pick, text_pick)


def solution(mesh):
    in_specs = (
        P("seq"),
        P("seq", None),
        P("seq"),
        P("seq", None),
        P(),
        P("seq", "vocab"),
        P("seq", "vocab"),
        P("seq", "vocab"),
    )
    out_specs = P("seq", "vocab")
    return jax.shard_map(
        on_device, mesh=mesh, in_specs=in_specs, out_specs=out_specs, check_vma=False
    )
```

profile of v0, /device:TPU:31, one launch (start us, length us, event | category | flops | bytes accessed | tf_op | source)
XLA Modules:
  0.0 121.0 jit_solution(3465705943747054290)
XLA Ops:
  0.7 1.2 %dynamic-slice = u32[1]{0:T(128)} dynamic-slice(u32[32]{0:T(128)} %constant.50, u32[]{:T(128)S(6)} %add.79), dynamic_slice_sizes={1} | dynamic-slice | bytes 12
  2.5 0.9 convert_reduce_fusion.1
  3.5 0.7 multiply_add_fusion.1
  4.1 0.7 and_select_fusion
  4.8 0.2 convert_reduce_fusion
  5.0 0.7 multiply_add_fusion
  5.7 0.7 broadcast_in_dim.25.gain_ref
  6.4 0.8 add_dynamic-update-slice_fusion
  7.1 4.4 %all-reduce = s32[1280]{0:T(1024)S(1)} all-reduce(s32[1280]{0:T(1024)S(1)} %add_dynamic-update-slice_fusion), channel_id=2, replica_groups=mesh['seq'=8,'vocab'=4] {'seq'}, use_global_device_ids=true, to_apply=%add | all-reduce | flops 1280 | bytes 10240
  11.6 0.1 reshape.99
  11.6 0.7 convert_reduce_fusion.2
  13.0 0.1 select_reduce_fusion.1
  13.1 0.1 add_select_fusion.2
  13.2 0.1 select_n.45
  13.3 0.3 reduce_window_sum.11
  13.5 0.2 select_reduce_fusion.ids_ref
  13.8 0.0 copy-start.4
  13.8 0.1 fusion.3.placed_ref
  13.9 0.8 fusion.pick_ref
  14.7 0.0 copy-done.4
  14.7 0.0 copy-start.1
  14.7 0.0 copy-start.3
  14.7 9.0 %gather_rows.1.text_ref = bf16[8,32,2048]{2,1,0:T(8,128)(2,1)} custom-call(s32[8,32]{1,0:T(8,128)} %copy-done.4, bf16[8,32,256]{2,1,0:T(8,128)(2,1)} %fusion.pick_ref, bf16[9504,2048]{1,0:T(8,128)(2,1)} %table_ref.1), custom_call_target="tpu_custom_call" | custom-call | tf_op jit(solution)/shard_map/gather_rows/pallas_call | solution.py:48
  23.7 0.0 copy-done.1
  23.7 0.0 copy-done.3
  23.7 0.0 copy-start
  23.8 1.2 %copy-done = bf16[8,32,2048]{2,1,0:T(8,128)(2,1)S(1)} copy-done((bf16[8,32,2048]{2,1,0:T(8,128)(2,1)S(1)}, bf16[8,32,2048]{2,1,0:T(8,128)(2,1)}, u32[]{:S(2)}) %copy-start) | copy-done | bytes 1048600
  25.0 0.0 copy-start.2
  25.0 1.4 %copy-done.2 = bf16[640,1280]{1,0:T(8,128)(2,1)S(1)} copy-done((bf16[640,1280]{1,0:T(8,128)(2,1)S(1)}, bf16[640,1280]{1,0:T(8,128)(2,1)}, u32[]{:S(2)}) %copy-start.2) | copy-done | bytes 1638424
  26.4 93.8 %merger.1 = bf16[128,2048]{1,0:T(8,128)(2,1)S(1)} custom-call(bf16[32,5120]{1,0:T(8,128)(2,1)S(1)} %copy-done.3, f32[1,1280]{1,0:T(1,128)S(1)} %broadcast_in_dim.25.gain_ref, bf16[640,1280]{1,0:T(8,128)(2,1)S(1)} %copy-done.2, bf16[640,2048]{1,0:T(8,128)(2,1)S(1)} %copy-done.1, bf16[8,32,2048]{2,1,0:T(8,128)(2,1)S(1)} %copy-done, ...), custom_call_target="tpu_custom_call" | custom-call | tf_op jit(solution)/shard_map/merger/pallas_call | solution.py:333
  120.2 0.8 copy.12
  (9 shorter events, 0.1 us)
Async XLA Ops:
  13.8 0.9 copy-start.4
  14.7 9.0 %copy-start.1 = (bf16[640,2048]{1,0:T(8,128)(2,1)S(1)}, bf16[640,2048]{1,0:T(8,128)(2,1)}, u32[]{:S(2)}) copy-start(bf16[640,2048]{1,0:T(8,128)(2,1)} %w2_hbm.1) | copy-start | bytes 7864324
  14.7 9.0 %copy-start.3 = (bf16[32,5120]{1,0:T(8,128)(2,1)S(1)}, bf16[32,5120]{1,0:T(8,128)(2,1)}, u32[]{:S(2)}) copy-start(bf16[32,5120]{1,0:T(8,128)(2,1)} %vision_ref.1) | copy-start | bytes 983044
  23.7 1.2 %copy-start = (bf16[8,32,2048]{2,1,0:T(8,128)(2,1)S(1)}, bf16[8,32,2048]{2,1,0:T(8,128)(2,1)}, u32[]{:S(2)}) copy-start(bf16[8,32,2048]{2,1,0:T(8,128)(2,1)} %gather_rows.1.text_ref) | copy-start | bytes 3145732
  25.0 1.4 %copy-start.2 = (bf16[640,1280]{1,0:T(8,128)(2,1)S(1)}, bf16[640,1280]{1,0:T(8,128)(2,1)}, u32[]{:S(2)}) copy-start(bf16[640,1280]{1,0:T(8,128)(2,1)} %w1_hbm.1) | copy-start | bytes 4915204
where the time goes:
time: 121 us
  Pallas kernels  103 us (85%)
  other arithmetic  6.13 us (5%)
  local copies, waits for them, and re-layouts  5.56 us (5%)
  blocking collectives  4.43 us (4%)
  between operations  2.08 us (2%)
    pallas_call x1, Pallas kernels, mega(): pl.pallas_call(mega_kernel, out_shape=jax.ShapeDtypeStruct((image_pick.sh...  93.8 us
    pallas_call x1, Pallas kernels, gather_rows(): pl.pallas_call(gather_kernel, out_shape=jax.ShapeDtypeStruct((groups, cap...  9.01 us
    unnamed x13, local copies, waits for them, and re-layouts  4.7 us
    unnamed x1, blocking collectives  4.43 us

commit v1 on v0

--- a/solution.py
+++ b/solution.py
@@ -111,10 +111,10 @@
 
 def mega_kernel(
     vision_ref, gain_ref, w1_hbm, w2_hbm, text_ref, selector_ref, image_ref, placed_ref, out_ref,
-    w1, w2, x_send, x_recv, half_send, half_recv, half_own, cross_send, cross_recv,
-    h_send, h_recv, pair_send, pair_recv, pair_own, part_send, part_recv,
+    w1, w2, x_send, x_recv, half_send, half_recv, half_own, plane_send, plane_recv, cross_recv,
+    h_own, h_recv, pair_send, pair_recv, pair_own, part_send, part_recv,
     row_send, row_recv, text_recv, total,
-    w_sem, x_sems, half_sems, cross_sems, h_send_sems, h_recv_sems,
+    w_sem, x_sems, half_sems, plane_sems, cross_sems, h_sems,
     pair_sems, part_sems, row_sems, text_sems,
 ):
     n, voc = lax.axis_size("seq"), lax.axis_size("vocab")
@@ -124,6 +124,7 @@
     split = n // voc
     f32, bf16 = jnp.float32, jnp.bfloat16
     slots = vision_ref.shape[0]
+    blocks, block = x_send.shape[1], x_send.shape[2]
 
     def at(seq, vocab):
         return dict(device_id=(seq, vocab), device_id_type=pl.DeviceIdType.MESH)
@@ -133,47 +134,47 @@
     load1.start()
     load2.start()
 
-    feeds = s // split
     barrier = pltpu.get_barrier_semaphore()
     for d in range(1, n):
         pl.semaphore_signal(barrier, inc=1, **at(lax.rem(s + d, n), v))
     for e in range(1, voc):
-        for j in range(split):
-            pl.semaphore_signal(barrier, inc=1, **at(v * split + j, lax.rem(v + e, voc)))
-
-    @pl.when(feeds != v)
-    def _():
-        for r in range(n):
-            pl.semaphore_signal(barrier, inc=1, **at(r, feeds))
+        pl.semaphore_signal(barrier, inc=1, **at(s, lax.rem(v + e, voc)))
 
     group = gain_ref.shape[1]
-    depth = x_send.shape[2]
+    depth = x_send.shape[3]
     for g in range(vision_ref.shape[1] // group):
         values = vision_ref[:, g * group : (g + 1) * group].astype(f32)
         center = values - jnp.mean(values, axis=-1, keepdims=True)
         spread = jnp.mean(center * center, axis=-1, keepdims=True)
         normed = (center / jnp.sqrt(spread + 1e-06) * gain_ref[...]).astype(bf16)
         for k in range(group // depth):
-            x_send[g * (group // depth) + k] = normed[:, k * depth : (k + 1) * depth]
-
-    pl.semaphore_wait(barrier, n - 1 + (voc - 1) * split + jnp.where(feeds != v, n, 0))
-
-    def to_peer(source, target, sems, d, seq):
+            part = normed[:, k * depth : (k + 1) * depth]
+            for i in range(blocks):
+                x_send[g * (group // depth) + k, i] = part[i * block : (i + 1) * block]
+
+    pl.semaphore_wait(barrier, n - 1 + voc - 1)
+
+    def to_peer(source, target, sems, d, seq, vocab=None):
         copy = pltpu.make_async_remote_copy(
             src_ref=source,
             dst_ref=target,
             send_sem=sems.at[0, d],
             recv_sem=sems.at[1, d],
-            **at(seq, v),
+            **at(seq, v if vocab is None else vocab),
         )
         copy.start()
         return copy
 
+    def x_place(seq):
+        if blocks == 1:
+            return x_recv.at[pl.ds(seq % 2, 1), seq // 2]
+        return x_recv.at[:, seq]
+
     copies = []
     for d in range(1, n):
         peer = lax.rem(s + d, n)
-        copies.append(to_peer(x_send.at[peer], x_recv.at[c, z], x_sems, d, peer))
-    x_recv[c, z] = x_send[s]
+        copies.append(to_peer(x_send.at[peer], x_place(s), x_sems, d, peer))
+    x_place(s)[...] = x_send[s]
 
     texts = []
 
@@ -190,12 +191,11 @@
     def columns(width):
         return 256 if width % 256 == 0 else width
 
-    def summed(lhs_ref, weight, to_sib, from_sib, own, send, recv, sems_pair, sems_part, ds):
+    def chip_sums(lhs_ref, weight, to_sib, from_sib, own, sems_pair):
         width = weight.shape[1]
         step = columns(width)
-        rows = chips * slots
         for core, keep in ((1 - c, False), (c, True)):
-            lhs = lhs_ref[core].reshape(rows, weight.shape[0])
+            lhs = lhs_ref[core].reshape(-1, weight.shape[0])
             for k in range(0, width, step):
                 part = jnp.dot(lhs, weight[:, k : k + step], preferred_element_type=f32)
                 if keep:
@@ -205,69 +205,72 @@
             if not keep:
                 swap = to_peer(to_sib, from_sib, sems_pair, 0, s + 1 - 2 * c)
         swap.wait()
-        sent = []
-        for d in range(1, chips):
-            other = lax.rem(z + d, chips)
-            span = pl.ds(pl.multiple_of(other * slots, slots), slots)
-            send[d] = (own[span, :] + from_sib[span, :].astype(f32)).astype(bf16)
-            sent.append(to_peer(send.at[d], recv.at[d], sems_part, d, other * 2 + c))
-        send_text(ds)
-        span = pl.ds(pl.multiple_of(z * slots, slots), slots)
-        value = own[span, :] + from_sib[span, :].astype(f32)
-        for copy in sent:
-            copy.wait()
-        for d in range(1, chips):
-            value = value + recv[d].astype(f32)
-        return value
 
     load1.wait()
-    pre = summed(x_recv, w1, half_send, half_recv, half_own, cross_send, cross_recv,
-                 half_sems, cross_sems, TEXT_B(n))
-    hidden = (0.5 * pre * (1.0 + lax.erf(pre * math.sqrt(0.5)))).astype(bf16)
-    inner = h_send.shape[2]
-    for j in range(split):
-        h_send[j] = hidden[:, j * inner : (j + 1) * inner]
-
-    def hidden_copy(e, j):
-        return pltpu.make_async_remote_copy(
-            src_ref=h_send.at[j],
-            dst_ref=h_recv.at[c, z],
-            send_sem=h_send_sems.at[e, j],
-            recv_sem=h_recv_sems.at[s],
-            **at(v * split + j, lax.rem(v + e, voc)),
-        )
-
-    for j in range(split):
-        target = v * split + j
-
-        @pl.when(target != s)
-        def _():
-            hidden_copy(0, j).start()
-
-        @pl.when(target == s)
-        def _():
-            h_recv[c, z] = h_send[j]
-
-        for e in range(1, voc):
-            hidden_copy(e, j).start()
+    chip_sums(x_recv, w1, half_send, half_recv, half_own, half_sems)
+    copies = []
+    for e in range(1, voc):
+        peer = lax.rem(v + e, voc)
+        span = pl.ds(pl.multiple_of(peer * block, block), block)
+        plane_send[e] = (half_own[span, :] + half_recv[span, :].astype(f32)).astype(bf16)
+        copies.append(to_peer(plane_send.at[e], plane_recv.at[v], plane_sems, e, s, peer))
+    send_text(TEXT_B(n))
+    span = pl.ds(pl.multiple_of(v * block, block), block)
+    plane_recv[v] = (half_own[span, :] + half_recv[span, :].astype(f32)).astype(bf16)
+    for copy in copies:
+        copy.wait()
+
+    inner = h_own.shape[2]
+
+    def hidden_part(seq):
+        side = pl.multiple_of(seq % split * inner, inner) if split > 1 else 0
+        return plane_recv.at[seq // split, :, pl.ds(side, inner)]
+
+    copies = []
+    for d in range(1, n):
+        peer = lax.rem(s + d, n)
+        copies.append(to_peer(hidden_part(peer), cross_recv.at[s], cross_sems, d, peer))
+    cross_recv[s] = hidden_part(s)[...]
     send_text(TEXT_C(n))
+    for copy in copies:
+        copy.wait()
+    for core in range(2):
+        pre = cross_recv[core].astype(f32)
+        for k in range(1, chips):
+            pre = pre + cross_recv[2 * k + core].astype(f32)
+        h_own[core] = (0.5 * pre * (1.0 + lax.erf(pre * math.sqrt(0.5)))).astype(bf16)
+
+    def h_place(vocab):
+        if blocks == 1:
+            return h_recv.at[:, vocab, 0]
+        return h_recv.at[vocab % 2, vocab // 2]
+
+    copies = []
+    for e in range(1, voc):
+        peer = lax.rem(v + e, voc)
+        copies.append(to_peer(h_own, h_place(v), h_sems, e, s, peer))
+    h_place(v)[...] = h_own[...]
     load2.wait()
-    for r in range(n):
-        def arrived():
-            pltpu.make_async_remote_copy(
-                src_ref=h_send.at[0],
-                dst_ref=h_recv.at[r % 2, r // 2],
-                send_sem=h_send_sems.at[0, 0],
-                recv_sem=h_recv_sems.at[r],
-                **at(lax.rem(s + 1, n), v),
-            ).wait_recv()
-
-        pl.when(jnp.logical_or(r != s, feeds != v))(arrived)
-
-    merged = summed(h_recv, w2, pair_send, pair_recv, pair_own, part_send, part_recv,
-                    pair_sems, part_sems, TEXT_D(n)).astype(bf16)
+    for copy in copies:
+        copy.wait()
 
     width = w2.shape[1]
+    chip_sums(h_recv, w2, pair_send, pair_recv, pair_own, pair_sems)
+    sent = []
+    for d in range(1, chips):
+        other = lax.rem(z + d, chips)
+        span = pl.ds(pl.multiple_of(other * slots, slots), slots)
+        part_send[d] = (pair_own[span, :] + pair_recv[span, :].astype(f32)).astype(bf16)
+        sent.append(to_peer(part_send.at[d], part_recv.at[d], part_sems, d, other * 2 + c))
+    send_text(TEXT_D(n))
+    span = pl.ds(pl.multiple_of(z * slots, slots), slots)
+    value = pair_own[span, :] + pair_recv[span, :].astype(f32)
+    for copy in sent:
+        copy.wait()
+    for d in range(1, chips):
+        value = value + part_recv[d].astype(f32)
+    merged = value.astype(bf16)
+
     cap = row_send.shape[1]
     outgoing = jnp.dot(selector_ref[...], merged, preferred_element_type=f32).astype(bf16)
     for t in range(n):
@@ -289,18 +292,9 @@
         copy.wait()
     for k in range(0, width, step):
         value = total[:, k : k + step]
-        block = row_recv[:, :, k : k + step].astype(f32).reshape(n * cap, step).astype(bf16)
-        value = value + jnp.dot(image_ref[...], block, preferred_element_type=f32)
+        block_rows = row_recv[:, :, k : k + step].astype(f32).reshape(n * cap, step).astype(bf16)
+        value = value + jnp.dot(image_ref[...], block_rows, preferred_element_type=f32)
         out_ref[:, k : k + step] = value.astype(bf16)
-    for j in range(split):
-        for e in range(voc):
-            def left():
-                hidden_copy(e, j).wait_send()
-
-            if e == 0:
-                pl.when(v * split + j != s)(left)
-            else:
-                left()
 
 
 def TEXT_A(n):
@@ -323,6 +317,8 @@
     n, voc = lax.axis_size("seq"), lax.axis_size("vocab")
     slots = vision.shape[0]
     rows = n // 2 * slots
+    block = n * slots // (2 * voc)
+    blocks = slots // block
     depth, mid = w1.shape
     inner, width = w2.shape
     cap = selector.shape[0] // n
@@ -338,15 +334,16 @@
         scratch_shapes=[
             pltpu.VMEM(w1.shape, bf16),
             pltpu.VMEM(w2.shape, bf16),
-            pltpu.VMEM((n, slots, depth), bf16),
-            pltpu.VMEM((2, n // 2, slots, depth), bf16),
-            pltpu.VMEM((rows, mid), bf16),
-            pltpu.VMEM((rows, mid), bf16),
-            pltpu.VMEM((rows, mid), f32),
-            pltpu.VMEM((n // 2, slots, mid), bf16),
-            pltpu.VMEM((n // 2, slots, mid), bf16),
-            pltpu.VMEM((n // voc, slots, inner), bf16),
-            pltpu.VMEM((2, n // 2, slots, inner), bf16),
+            pltpu.VMEM((n, blocks, block, depth), bf16),
+            pltpu.VMEM((2, voc, block, depth), bf16),
+            pltpu.VMEM((voc * block, mid), bf16),
+            pltpu.VMEM((voc * block, mid), bf16),
+            pltpu.VMEM((voc * block, mid), f32),
+            pltpu.VMEM((voc, block, mid), bf16),
+            pltpu.VMEM((voc, block, mid), bf16),
+            pltpu.VMEM((n, block, inner), bf16),
+            pltpu.VMEM((2, block, inner), bf16),
+            pltpu.VMEM((2, n // 2, blocks, block, inner), bf16),
             pltpu.VMEM((rows, width), bf16),
             pltpu.VMEM((rows, width), bf16),
             pltpu.VMEM((rows, width), f32),
@@ -359,9 +356,9 @@
             dma((2,)),
             dma((2, n)),
             dma((2, 1)),
-            dma((2, n // 2)),
-            dma((voc, n // voc)),
-            dma((n,)),
+            dma((2, voc)),
+            dma((2, n)),
+            dma((2, voc)),
             dma((2, 1)),
             dma((2, n // 2)),
             dma((2, n)),

time: 121 us -> 103 us (0.85)
  the two profiles are of different devices: /device:TPU:31 before, /device:TPU:0 now
where the time goes in v1:
time: 103 us; the launch traced here: 102 us
  Pallas kernels  77.4 us (75%)
  blocking collectives  10.8 us (10%)
  other arithmetic  6.14 us (6%)
  local copies, waits for them, and re-layouts  5.56 us (5%)
  between operations  2.07 us (2%)
    pallas_call x1, Pallas kernels, mega(): pl.pallas_call(mega_kernel, out_shape=jax.ShapeDtypeStruct((image_pick.sh...  68.4 us
    unnamed x1, blocking collectives  10.8 us
    pallas_call x1, Pallas kernels, gather_rows(): pl.pallas_call(gather_kernel, out_shape=jax.ShapeDtypeStruct((groups, cap...  9.05 us
    unnamed x13, local copies, waits for them, and re-layouts  4.7 us

profile of v1, /device:TPU:0, one launch (start us, length us, event | category | flops | bytes accessed | tf_op | source)
XLA Modules:
  0.0 102.0 jit_solution(3069337250162819253)
XLA Ops:
  0.7 1.2 %dynamic-slice = u32[1]{0:T(128)} dynamic-slice(u32[32]{0:T(128)} %constant.50, u32[]{:T(128)S(6)} %add.79), dynamic_slice_sizes={1} | dynamic-slice | bytes 12
  2.5 0.9 convert_reduce_fusion.1
  3.5 0.7 multiply_add_fusion.1
  4.1 0.7 and_select_fusion
  4.8 0.2 convert_reduce_fusion
  5.0 0.7 multiply_add_fusion
  5.7 0.7 broadcast_in_dim.25.gain_ref
  6.4 0.8 add_dynamic-update-slice_fusion
  7.1 10.8 %all-reduce = s32[1280]{0:T(1024)S(1)} all-reduce(s32[1280]{0:T(1024)S(1)} %add_dynamic-update-slice_fusion), channel_id=2, replica_groups=mesh['seq'=8,'vocab'=4] {'seq'}, use_global_device_ids=true, to_apply=%add | all-reduce | flops 1280 | bytes 10240
  17.9 0.1 reshape.99
  18.0 0.7 convert_reduce_fusion.2
  19.3 0.1 select_reduce_fusion.1
  19.4 0.1 add_select_fusion.2
  19.5 0.1 select_n.45
  19.6 0.3 reduce_window_sum.11
  19.9 0.2 select_reduce_fusion.ids_ref
  20.1 0.0 copy-start.4
  20.2 0.1 fusion.3.placed_ref
  20.3 0.8 fusion.pick_ref
  21.0 0.0 copy-done.4
  21.0 0.0 copy-start.1
  21.1 0.0 copy-start.3
  21.1 9.1 %gather_rows.1.text_ref = bf16[8,32,2048]{2,1,0:T(8,128)(2,1)} custom-call(s32[8,32]{1,0:T(8,128)} %copy-done.4, bf16[8,32,256]{2,1,0:T(8,128)(2,1)} %fusion.pick_ref, bf16[9504,2048]{1,0:T(8,128)(2,1)} %table_ref.1), custom_call_target="tpu_custom_call" | custom-call | tf_op jit(solution)/shard_map/gather_rows/pallas_call | solution.py:48
  30.1 0.0 copy-done.1
  30.1 0.0 copy-done.3
  30.1 0.0 copy-start
  30.1 1.2 %copy-done = bf16[8,32,2048]{2,1,0:T(8,128)(2,1)S(1)} copy-done((bf16[8,32,2048]{2,1,0:T(8,128)(2,1)S(1)}, bf16[8,32,2048]{2,1,0:T(8,128)(2,1)}, u32[]{:S(2)}) %copy-start) | copy-done | bytes 1048600
  31.4 0.0 copy-start.2
  31.4 1.4 %copy-done.2 = bf16[640,1280]{1,0:T(8,128)(2,1)S(1)} copy-done((bf16[640,1280]{1,0:T(8,128)(2,1)S(1)}, bf16[640,1280]{1,0:T(8,128)(2,1)}, u32[]{:S(2)}) %copy-start.2) | copy-done | bytes 1638424
  32.8 68.4 %merger.1 = bf16[128,2048]{1,0:T(8,128)(2,1)S(1)} custom-call(bf16[32,5120]{1,0:T(8,128)(2,1)S(1)} %copy-done.3, f32[1,1280]{1,0:T(1,128)S(1)} %broadcast_in_dim.25.gain_ref, bf16[640,1280]{1,0:T(8,128)(2,1)S(1)} %copy-done.2, bf16[640,2048]{1,0:T(8,128)(2,1)S(1)} %copy-done.1, bf16[8,32,2048]{2,1,0:T(8,128)(2,1)S(1)} %copy-done, ...), custom_call_target="tpu_custom_call" | custom-call | tf_op jit(solution)/shard_map/merger/pallas_call | solution.py:329
  101.2 0.8 copy.12
  (9 shorter events, 0.1 us)
Async XLA Ops:
  20.1 0.9 copy-start.4
  21.0 9.1 %copy-start.1 = (bf16[640,2048]{1,0:T(8,128)(2,1)S(1)}, bf16[640,2048]{1,0:T(8,128)(2,1)}, u32[]{:S(2)}) copy-start(bf16[640,2048]{1,0:T(8,128)(2,1)} %w2_hbm.1) | copy-start | bytes 7864324
  21.1 9.1 %copy-start.3 = (bf16[32,5120]{1,0:T(8,128)(2,1)S(1)}, bf16[32,5120]{1,0:T(8,128)(2,1)}, u32[]{:S(2)}) copy-start(bf16[32,5120]{1,0:T(8,128)(2,1)} %vision_ref.1) | copy-start | bytes 983044
  30.1 1.2 %copy-start = (bf16[8,32,2048]{2,1,0:T(8,128)(2,1)S(1)}, bf16[8,32,2048]{2,1,0:T(8,128)(2,1)}, u32[]{:S(2)}) copy-start(bf16[8,32,2048]{2,1,0:T(8,128)(2,1)} %gather_rows.1.text_ref) | copy-start | bytes 3145732
  31.4 1.4 %copy-start.2 = (bf16[640,1280]{1,0:T(8,128)(2,1)S(1)}, bf16[640,1280]{1,0:T(8,128)(2,1)}, u32[]{:S(2)}) copy-start(bf16[640,1280]{1,0:T(8,128)(2,1)} %w1_hbm.1) | copy-start | bytes 4915204

commit v2 on v1

v2 whole, which is shorter than its diff:
```python
import math

import jax
import jax.numpy as jnp
from jax import lax
from jax.experimental import pallas as pl
from jax.experimental.pallas import tpu as pltpu
from jax.sharding import PartitionSpec as P


PAIR = 2
LANES = 128


def at(seq, vocab):
    return dict(device_id=(seq, vocab), device_id_type=pl.DeviceIdType.MESH)


def iota(shape, dim):
    return lax.broadcasted_iota(jnp.int32, shape, dim)


def x_slot(ref, seq, blocks):
    if blocks == 1:
        return ref.at[pl.ds(seq % 2, 1), seq // 2]
    return ref.at[:, seq]


def exchange_kernel(
    shard_rows, ids_ref, routes_ref, start_ref, vision_ref, gain_ref,
    local_ref, pick_ref, selector_ref, image_ref, placed_ref, x_ref,
    pack, pack_recv, x_send, x_recv, id_sems, x_sems,
):
    n = lax.axis_size("seq")
    s, v = lax.axis_index("seq"), lax.axis_index("vocab")
    f32, bf16, i32 = jnp.float32, jnp.bfloat16, jnp.int32
    tokens, slots = ids_ref.shape[1], routes_ref.shape[1]
    id_cap = local_ref.shape[1]
    cap = selector_ref.shape[0] // n
    blocks, block, depth = x_send.shape[1:]

    barrier = pltpu.get_barrier_semaphore()
    for d in range(1, n):
        pl.semaphore_signal(barrier, inc=1, **at(lax.rem(s + d, n), v))

    pack[...] = jnp.full(pack.shape, -1, i32)
    pack[0:1, :tokens] = ids_ref[...]
    pack[1:2, :slots] = routes_ref[...]
    pack_recv[s] = pack[...]

    group = gain_ref.shape[1]
    for g in range(vision_ref.shape[1] // group):
        values = vision_ref[:, g * group : (g + 1) * group].astype(f32)
        center = values - jnp.mean(values, axis=-1, keepdims=True)
        spread = jnp.mean(center * center, axis=-1, keepdims=True)
        normed = (center / jnp.sqrt(spread + 1e-06) * gain_ref[...]).astype(bf16)
        for k in range(group // depth):
            part = normed[:, k * depth : (k + 1) * depth]
            for i in range(blocks):
                x_send[g * (group // depth) + k, i] = part[i * block : (i + 1) * block]

    pl.semaphore_wait(barrier, n - 1)

    def to_peer(source, target, sems, d, seq):
        copy = pltpu.make_async_remote_copy(
            src_ref=source,
            dst_ref=target,
            send_sem=sems.at[0, d],
            recv_sem=sems.at[1, d],
            **at(seq, v),
        )
        copy.start()
        return copy

    id_copies, x_copies = [], []
    for d in range(1, n):
        peer = lax.rem(s + d, n)
        id_copies.append(to_peer(pack, pack_recv.at[s], id_sems, d, peer))
    for d in range(1, n):
        peer = lax.rem(s + d, n)
        x_copies.append(
            to_peer(x_send.at[peer], x_slot(x_recv, s, blocks), x_sems, d, peer)
        )
    x_slot(x_recv, s, blocks)[...] = x_send[s]

    lane_t = iota((tokens, tokens), 1)
    upto = (iota((tokens, tokens), 0) <= lane_t).astype(bf16)
    before = (iota((tokens, tokens), 0) < lane_t).astype(bf16)

    own = ids_ref[...]
    home = jnp.zeros((1, tokens), i32)
    for r in range(1, n):
        home = home + (own >= r * shard_rows).astype(i32)
    home_hot = home == iota((n, tokens), 0)
    ahead = jnp.dot(home_hot.astype(bf16), before, preferred_element_type=f32)
    rank = jnp.sum(jnp.where(home_hot, ahead, 0.0), axis=0, keepdims=True)
    arrive = home.astype(f32) * id_cap + rank
    arrive = jnp.transpose(jnp.broadcast_to(arrive, (8, tokens)))[:, 0:1].astype(i32)

    owner = pack[1:2, :]
    owner_hot = owner == iota((n, LANES), 0)
    before_slot = (iota((LANES, LANES), 0) < iota((LANES, LANES), 1)).astype(bf16)
    ahead = jnp.dot(owner_hot.astype(bf16), before_slot, preferred_element_type=f32)
    rank = jnp.sum(jnp.where(owner_hot, ahead, 0.0), axis=0, keepdims=True)
    slot_of = owner * cap + rank.astype(i32)
    selector = (slot_of == iota((n * cap, LANES), 0)).astype(f32)
    selector_ref[...] = selector[:, :slots].astype(bf16)

    for copy in id_copies:
        copy.wait()
    everyone = pack_recv[...]
    all_ids, all_routes = everyone[:, 0, :tokens], everyone[:, 1, :]
    relative = all_ids - s * shard_rows
    mine = (relative >= 0) & (relative < shard_rows)
    relative = jnp.where(mine, relative, 0)
    place = jnp.dot(mine.astype(bf16), upto, preferred_element_type=f32).astype(i32) - 1
    place = jnp.where(mine, place, -1)
    high, low = relative // LANES, relative % LANES
    found_high = jnp.zeros((n, id_cap), f32)
    found_low = jnp.zeros((n, id_cap), f32)
    row_n = iota((n, id_cap), 0)
    for t in range(n):
        hot = place[t : t + 1, :] == iota((id_cap, tokens), 0)
        hot_f = hot.astype(bf16)
        pick_dims = (((1,), (1,)), ((), ()))
        part = lax.dot_general(high.astype(bf16), hot_f, pick_dims, preferred_element_type=f32)
        found_high = jnp.where(row_n == t, part, found_high)
        part = lax.dot_general(low.astype(bf16), hot_f, pick_dims, preferred_element_type=f32)
        found_low = jnp.where(row_n == t, part, found_low)
        odd = jnp.sum(jnp.where(hot, relative[t : t + 1, :] % PAIR, 0).astype(f32), axis=1, keepdims=True)
        first = t * id_cap % (pick_ref.shape[1] // PAIR)
        rows = first + iota((id_cap, pick_ref.shape[1]), 0)
        chosen = rows * PAIR + odd.astype(i32) == iota((id_cap, pick_ref.shape[1]), 1)
        pick_ref[t * id_cap : (t + 1) * id_cap, :] = chosen.astype(f32).astype(bf16)
    local_ref[...] = (found_high * LANES + found_low).astype(i32)

    counts = jnp.sum((all_routes == s).astype(f32), axis=1, keepdims=True)
    spots = image_ref.shape[1]
    sender = iota((n, LANES), 1) // cap
    count_of = jnp.sum(jnp.where(sender == iota((n, LANES), 0), counts, 0.0), axis=0, keepdims=True)
    offset_of = jnp.sum(jnp.where(sender > iota((n, LANES), 0), counts, 0.0), axis=0, keepdims=True)
    within = iota((1, LANES), 1) % cap
    start = start_ref[0]
    position = jnp.where(
        within < count_of.astype(i32), start + offset_of.astype(i32) + within, -1
    )
    image = (position == iota((tokens, LANES), 0)).astype(f32)
    image_ref[...] = image[:, :spots].astype(bf16)
    total = jnp.sum(counts).astype(i32)
    row = iota((tokens, placed_ref.shape[1]), 0)
    is_text = (row < start) | (row >= start + total)
    hot = (arrive == iota((tokens, placed_ref.shape[1]), 1)) & is_text
    placed_ref[...] = hot.astype(f32).astype(bf16)

    for copy in x_copies:
        copy.wait()
    x_ref[...] = x_recv[...]


def exchange(token_ids, routes, splice_start, vision, gain, table_rows, depth):
    n, voc = lax.axis_size("seq"), lax.axis_size("vocab")
    tokens, slots = token_ids.shape[0], routes.shape[0]
    block = n * slots // (2 * voc)
    blocks = slots // block
    id_cap, cap = 2 * tokens // n, 2 * slots // n
    i32, bf16 = jnp.int32, jnp.bfloat16
    vmem = pl.BlockSpec(memory_space=pltpu.VMEM)
    smem = pl.BlockSpec(memory_space=pltpu.SMEM)
    dma = pltpu.SemaphoreType.DMA
    shape = jax.ShapeDtypeStruct
    held = PAIR * min(n * id_cap, 128)

    def body(*refs):
        exchange_kernel(table_rows, *refs)

    return pl.pallas_call(
        body,
        out_shape=(
            shape((n, id_cap), i32),
            shape((n * id_cap, held), bf16),
            shape((n * cap, slots), bf16),
            shape((tokens, n * cap), bf16),
            shape((tokens, n * id_cap), bf16),
            shape((2, voc, block, depth), bf16),
        ),
        in_specs=[vmem, vmem, smem, vmem, vmem],
        out_specs=(vmem,) * 6,
        scratch_shapes=[
            pltpu.VMEM((8, LANES), i32),
            pltpu.VMEM((n, 8, LANES), i32),
            pltpu.VMEM((n, blocks, block, depth), bf16),
            pltpu.VMEM((2, voc, block, depth), bf16),
            dma((2, n)),
            dma((2, n)),
        ],
        compiler_params=pltpu.CompilerParams(
            collective_id=1, has_side_effects=True, vmem_limit_bytes=16 * 1024 * 1024
        ),
        name="exchange",
    )(token_ids[None, :], routes.reshape(1, slots), splice_start, vision, gain[None, :])


def gather_kernel(ids_ref, pick_ref, table_ref, out_ref, held, sems):
    groups, cap = ids_ref.shape
    span = pick_ref.shape[1]
    per = span // (PAIR * cap)

    def issue(g, carry):
        for k in range(cap):
            row = pl.multiple_of(ids_ref[g, k] // PAIR * PAIR, PAIR)
            spot = pl.multiple_of((g * cap + k) * PAIR, PAIR)
            pltpu.make_async_copy(
                table_ref.at[pl.ds(row, PAIR), :], held.at[pl.ds(spot, PAIR), :], sems.at[g // per]
            ).start()
        return carry

    lax.fori_loop(0, groups, issue, 0)

    for g in range(groups // per):
        block = held.at[g * span : (g + 1) * span, :]
        pltpu.make_async_copy(block, block, sems.at[g]).wait()
        rows = slice(g * per * cap, (g + 1) * per * cap)
        for k in range(0, held.shape[1], 256):
            found = jnp.dot(
                pick_ref[rows, :], block[:, k : k + 256], preferred_element_type=jnp.float32
            )
            out_ref[rows, k : k + 256] = found.astype(out_ref.dtype)


def gather_rows(local_ids, pick, table):
    groups, cap = local_ids.shape
    width = table.shape[1]
    found = pl.pallas_call(
        gather_kernel,
        out_shape=jax.ShapeDtypeStruct((groups * cap, width), table.dtype),
        in_specs=[
            pl.BlockSpec(memory_space=pltpu.SMEM),
            pl.BlockSpec(memory_space=pltpu.VMEM),
            pl.BlockSpec(memory_space=pl.ANY),
        ],
        out_specs=pl.BlockSpec(memory_space=pltpu.VMEM),
        scratch_shapes=[
            pltpu.VMEM((groups * cap * PAIR, width), table.dtype),
            pltpu.SemaphoreType.DMA((groups * cap * PAIR // pick.shape[1],)),
        ],
        name="gather_rows",
    )(local_ids, pick, table)
    return found.reshape(groups, cap, width)


def mega_kernel(
    x_ref, w1_hbm, w2_hbm, text_ref, selector_ref, image_ref, placed_ref, out_ref,
    w1, w2, half_send, half_recv, half_own, plane_send, plane_recv, cross_recv,
    h_own, h_recv, pair_send, pair_recv, pair_own, part_send, part_recv,
    row_send, row_recv, text_recv, total,
    w_sem, half_sems, plane_sems, cross_sems, h_sems,
    pair_sems, part_sems, row_sems, text_sems,
):
    n, voc = lax.axis_size("seq"), lax.axis_size("vocab")
    s, v = lax.axis_index("seq"), lax.axis_index("vocab")
    chips = n // 2
    z, c = s // 2, s % 2
    split = n // voc
    f32, bf16 = jnp.float32, jnp.bfloat16
    block = x_ref.shape[2]
    slots = voc * block // chips
    blocks = slots // block

    load1 = pltpu.make_async_copy(w1_hbm, w1, w_sem.at[0])
    load2 = pltpu.make_async_copy(w2_hbm, w2, w_sem.at[1])
    load1.start()
    load2.start()

    barrier = pltpu.get_barrier_semaphore()
    for d in range(1, n):
        pl.semaphore_signal(barrier, inc=1, **at(lax.rem(s + d, n), v))
    for e in range(1, voc):
        pl.semaphore_signal(barrier, inc=1, **at(s, lax.rem(v + e, voc)))

    pl.semaphore_wait(barrier, n - 1 + voc - 1)

    def to_peer(source, target, sems, d, seq, vocab=None):
        copy = pltpu.make_async_remote_copy(
            src_ref=source,
            dst_ref=target,
            send_sem=sems.at[0, d],
            recv_sem=sems.at[1, d],
            **at(seq, v if vocab is None else vocab),
        )
        copy.start()
        return copy

    texts = []

    def send_text(ds):
        for d in ds:
            peer = lax.rem(s + d, n)
            texts.append(to_peer(text_ref.at[peer], text_recv.at[s], text_sems, d, peer))

    send_text(TEXT_A(n))
    stay = pltpu.make_async_copy(text_ref.at[s], text_recv.at[s], w_sem.at[2])
    stay.start()

    def columns(width):
        return 256 if width % 256 == 0 else width

    def chip_sums(lhs_ref, weight, to_sib, from_sib, own, sems_pair):
        width = weight.shape[1]
        step = columns(width)
        for core, keep in ((1 - c, False), (c, True)):
            lhs = lhs_ref[core].reshape(-1, weight.shape[0])
            for k in range(0, width, step):
                part = jnp.dot(lhs, weight[:, k : k + step], preferred_element_type=f32)
                if keep:
                    own[:, k : k + step] = part
                else:
                    to_sib[:, k : k + step] = part.astype(bf16)
            if not keep:
                swap = to_peer(to_sib, from_sib, sems_pair, 0, s + 1 - 2 * c)
        swap.wait()

    load1.wait()
    chip_sums(x_ref, w1, half_send, half_recv, half_own, half_sems)
    copies = []
    for e in range(1, voc):
        peer = lax.rem(v + e, voc)
        span = pl.ds(pl.multiple_of(peer * block, block), block)
        plane_send[e] = (half_own[span, :] + half_recv[span, :].astype(f32)).astype(bf16)
        copies.append(to_peer(plane_send.at[e], plane_recv.at[v], plane_sems, e, s, peer))
    send_text(TEXT_B(n))
    span = pl.ds(pl.multiple_of(v * block, block), block)
    plane_recv[v] = (half_own[span, :] + half_recv[span, :].astype(f32)).astype(bf16)
    for copy in copies:
        copy.wait()

    inner = h_own.shape[2]

    def hidden_part(seq):
        side = pl.multiple_of(seq % split * inner, inner) if split > 1 else 0
        return plane_recv.at[seq // split, :, pl.ds(side, inner)]

    copies = []
    for d in range(1, n):
        peer = lax.rem(s + d, n)
        copies.append(to_peer(hidden_part(peer), cross_recv.at[s], cross_sems, d, peer))
    cross_recv[s] = hidden_part(s)[...]
    send_text(TEXT_C(n))
    for copy in copies:
        copy.wait()
    for core in range(2):
        pre = cross_recv[core].astype(f32)
        for k in range(1, chips):
            pre = pre + cross_recv[2 * k + core].astype(f32)
        h_own[core] = (0.5 * pre * (1.0 + lax.erf(pre * math.sqrt(0.5)))).astype(bf16)

    def h_place(vocab):
        if blocks == 1:
            return h_recv.at[:, vocab, 0]
        return h_recv.at[vocab % 2, vocab // 2]

    copies = []
    for e in range(1, voc):
        peer = lax.rem(v + e, voc)
        copies.append(to_peer(h_own, h_place(v), h_sems, e, s, peer))
    h_place(v)[...] = h_own[...]
    load2.wait()
    for copy in copies:
        copy.wait()

    width = w2.shape[1]
    chip_sums(h_recv, w2, pair_send, pair_recv, pair_own, pair_sems)
    sent = []
    for d in range(1, chips):
        other = lax.rem(z + d, chips)
        span = pl.ds(pl.multiple_of(other * slots, slots), slots)
        part_send[d] = (pair_own[span, :] + pair_recv[span, :].astype(f32)).astype(bf16)
        sent.append(to_peer(part_send.at[d], part_recv.at[d], part_sems, d, other * 2 + c))
    send_text(TEXT_D(n))
    span = pl.ds(pl.multiple_of(z * slots, slots), slots)
    value = pair_own[span, :] + pair_recv[span, :].astype(f32)
    for copy in sent:
        copy.wait()
    for d in range(1, chips):
        value = value + part_recv[d].astype(f32)
    merged = value.astype(bf16)

    cap = row_send.shape[1]
    outgoing = jnp.dot(selector_ref[...], merged, preferred_element_type=f32).astype(bf16)
    for t in range(n):
        row_send[t] = outgoing[t * cap : (t + 1) * cap]
    copies = []
    for d in range(1, n):
        peer = lax.rem(s + d, n)
        copies.append(to_peer(row_send.at[peer], row_recv.at[s], row_sems, d, peer))
    row_recv[s] = row_send[s]
    for copy in texts:
        copy.wait()
    stay.wait()
    step = columns(width)
    found = text_recv[...].reshape(-1, width)
    for k in range(0, width, step):
        total[:, k : k + step] = jnp.dot(
            placed_ref[...], found[:, k : k + step], preferred_element_type=f32
        )
    for copy in copies:
        copy.wait()
    for k in range(0, width, step):
        value = total[:, k : k + step]
        block_rows = row_recv[:, :, k : k + step].astype(f32).reshape(n * cap, step).astype(bf16)
        value = value + jnp.dot(image_ref[...], block_rows, preferred_element_type=f32)
        out_ref[:, k : k + step] = value.astype(bf16)


def TEXT_A(n):
    return range(1, 2)


def TEXT_B(n):
    return range(2, n // 2)


def TEXT_C(n):
    return range(n // 2, 3 * n // 4)


def TEXT_D(n):
    return range(3 * n // 4, n)


def mega(x, w1, w2, text, selector, image_pick, text_pick):
    n, voc = lax.axis_size("seq"), lax.axis_size("vocab")
    block = x.shape[2]
    slots = 2 * voc * block // n
    rows = n // 2 * slots
    blocks = slots // block
    depth, mid = w1.shape
    inner, width = w2.shape
    cap = selector.shape[0] // n
    bf16, f32 = jnp.bfloat16, jnp.float32
    vmem = pl.BlockSpec(memory_space=pltpu.VMEM)
    hbm = pl.BlockSpec(memory_space=pl.ANY)
    dma = pltpu.SemaphoreType.DMA
    return pl.pallas_call(
        mega_kernel,
        out_shape=jax.ShapeDtypeStruct((image_pick.shape[0], width), bf16),
        in_specs=[vmem, hbm, hbm, hbm, vmem, vmem, vmem],
        out_specs=vmem,
        scratch_shapes=[
            pltpu.VMEM(w1.shape, bf16),
            pltpu.VMEM(w2.shape, bf16),
            pltpu.VMEM((voc * block, mid), bf16),
            pltpu.VMEM((voc * block, mid), bf16),
            pltpu.VMEM((voc * block, mid), f32),
            pltpu.VMEM((voc, block, mid), bf16),
            pltpu.VMEM((voc, block, mid), bf16),
            pltpu.VMEM((n, block, inner), bf16),
            pltpu.VMEM((2, block, inner), bf16),
            pltpu.VMEM((2, n // 2, blocks, block, inner), bf16),
            pltpu.VMEM((rows, width), bf16),
            pltpu.VMEM((rows, width), bf16),
            pltpu.VMEM((rows, width), f32),
            pltpu.VMEM((n // 2, slots, width), bf16),
            pltpu.VMEM((n // 2, slots, width), bf16),
            pltpu.VMEM((n, cap, width), bf16),
            pltpu.VMEM((n, cap, width), bf16),
            pltpu.VMEM(text.shape, bf16),
            pltpu.VMEM((image_pick.shape[0], width), f32),
            dma((3,)),
            dma((2, 1)),
            dma((2, voc)),
            dma((2, n)),
            dma((2, voc)),
            dma((2, 1)),
            dma((2, n // 2)),
            dma((2, n)),
            dma((2, n)),
        ],
        compiler_params=pltpu.CompilerParams(
            collective_id=0, has_side_effects=True, vmem_limit_bytes=56 * 1024 * 1024
        ),
        name="merger",
    )(x, w1, w2, text, selector, image_pick, text_pick)


def on_device(token_ids, routes, splice_start, vision, ln_gain, table, w_fc1, w_fc2):
    local_ids, pick, selector, image_pick, text_pick, x = exchange(
        token_ids, routes, splice_start, vision, ln_gain, table.shape[0], w_fc1.shape[0]
    )
    text = gather_rows(local_ids, pick, table)
    return mega(x, w_fc1, w_fc2, text, selector, image_pick, text_pick)


def solution(mesh):
    in_specs = (
        P("seq"),
        P("seq", None),
        P("seq"),
        P("seq", None),
        P(),
        P("seq", "vocab"),
        P("seq", "vocab"),
        P("seq", "vocab"),
    )
    out_specs = P("seq", "vocab")
    return jax.shard_map(
        on_device, mesh=mesh, in_specs=in_specs, out_specs=out_specs, check_vma=False
    )
```

time: 103 us -> 93.1 us (0.904)
  blocking collectives: 10.8 us -> 0 us
  Pallas kernels: 77.4 us -> 83.8 us
  other arithmetic: 6.14 us -> 0 us
  local copies, waits for them, and re-layouts: 5.56 us -> 8.64 us
  between operations: 2.07 us -> 0.69 us
    unnamed x1 -> x0, blocking collectives: 10.8 us -> none
    pallas_call x1 -> x2, Pallas kernels: 9.05 us -> 19.4 us  [the longest x1 12 us: exchange(): pl.pallas_call(body, out_shape=(shape((n, id_cap), i32), shape((n * id_ca...]
    pallas_call x1, Pallas kernels: 68.4 us -> 64.4 us  [mega(): pl.pallas_call(mega_kernel, out_shape=jax.ShapeDtypeStruct((image_pick.sh...]
    unnamed x13 -> x19, local copies, waits for them, and re-layouts: 4.7 us -> 7.94 us
    reduce_sum x5 -> x0, other arithmetic: 2.07 us -> none  [the longest x1 0.91 us: route_plan(): slot_of = own * pair_cap + jnp.sum(earlier.astype(jnp.int32), axis=1)]
    add x4 -> x0, other arithmetic: 1.36 us -> none  [the longest x1 0.68 us: route_plan(): arrive = home * id_cap + jnp.sum(same.astype(jnp.int32), axis=1)]
where the time goes in v2:
time: 93.1 us
  Pallas kernels  83.8 us (90%)
  local copies, waits for them, and re-layouts  8.64 us (9%)
    pallas_call x1, Pallas kernels, mega(): pl.pallas_call(mega_kernel, out_shape=jax.ShapeDtypeStruct((image_pick.sh...  64.4 us
    pallas_call x1, Pallas kernels, exchange(): pl.pallas_call(body, out_shape=(shape((n, id_cap), i32), shape((n * id_ca...  12 us
    unnamed x19, local copies, waits for them, and re-layouts  7.94 us
    pallas_call x1, Pallas kernels, gather_rows(): pl.pallas_call(gather_kernel, out_shape=jax.ShapeDtypeStruct((groups * ca...  7.4 us

profile of v2, /device:TPU:0, one launch (start us, length us, event | category | flops | bytes accessed | tf_op | source)
XLA Modules:
  0.0 93.1 jit_solution(1875978140701091156)
XLA Ops:
  0.7 0.7 broadcast_in_dim.7.refs_4_
  1.4 0.0 copy-start.1
  1.4 1.0 %copy-done.1 = bf16[32,5120]{1,0:T(8,128)(2,1)S(1)} copy-done((bf16[32,5120]{1,0:T(8,128)(2,1)S(1)}, bf16[32,5120]{1,0:T(8,128)(2,1)}, u32[]{:S(2)}) %copy-start.1) | copy-done | bytes 327704
  2.3 0.0 copy-start.7
  2.3 0.7 copy-done.7
  3.0 0.0 copy-start.8
  3.0 0.7 copy-done.8
  3.6 12.0 %exchange.1 = (s32[8,32]{1,0:T(8,128)S(1)}, bf16[256,256]{1,0:T(8,128)(2,1)S(1)}, bf16[64,32]{1,0:T(8,128)(2,1)S(1)}, bf16[128,64]{1,0:T(8,128)(2,1)S(1)}, bf16[...) custom-call(s32[1,128]{1,0:T(1,128)S(1)} %bitcast.3, s32[1,32]{1,0:T(1,128)S(1)} %bitcast.4, ...), custom_call_target="tpu_custom_call" | custom-call | tf_op jit(solution)/shard_map/exchange/pallas_call | solution.py:176
  15.7 0.0 copy-start
  15.7 0.7 copy-done
  16.4 0.0 copy-start.2
  16.4 0.7 copy-done.2
  17.0 0.0 copy-start.3
  17.0 0.6 copy-done.3
  17.7 0.0 copy-start.4
  17.7 0.6 copy-done.4
  18.3 0.0 copy-start.5
  18.3 0.6 copy-done.5
  18.9 0.0 copy-start.6
  18.9 0.6 copy-done.6
  19.4 7.4 %gather_rows.1 = bf16[256,2048]{1,0:T(8,128)(2,1)} custom-call(s32[8,32]{1,0:T(8,128)} %copy-done.6, bf16[256,256]{1,0:T(8,128)(2,1)} %copy-done.2, bf16[9504,2048]{1,0:T(8,128)(2,1)} %table_ref.1), custom_call_target="tpu_custom_call" | custom-call | tf_op jit(solution)/shard_map/gather_rows/pallas_call | solution.py:233
  26.8 64.4 %merger.1 = bf16[128,2048]{1,0:T(8,128)(2,1)} custom-call(bf16[2,4,32,640]{3,2,1,0:T(8,128)(2,1)} %copy-done, bf16[640,1280]{1,0:T(8,128)(2,1)} %w1_hbm.1, bf16[640,2048]{1,0:T(8,128)(2,1)} %w2_hbm.1, bf16[8,32,2048]{2,1,0:T(8,128)(2,1)} %bitcast.5, bf16[64,32]{1,0:T(8,128)(2,1)} %copy-done.5, bf16[128,64]{1,0:T(8,128)(2,1)} %copy-done.4, ...), custom_call_target="tpu_custom_call" | custom-call | tf_op jit(solution)/shard_map/merger/pallas_call | solution.py:443
  91.2 1.9 %copy.11 = bf16[128,2048]{1,0:T(8,128)(2,1)} copy(bf16[128,2048]{1,0:T(8,128)(2,1)} %merger.1) | data formatting | bytes 1048576
Async XLA Ops:
  1.4 1.0 %copy-start.1 = (bf16[32,5120]{1,0:T(8,128)(2,1)S(1)}, bf16[32,5120]{1,0:T(8,128)(2,1)}, u32[]{:S(2)}) copy-start(bf16[32,5120]{1,0:T(8,128)(2,1)} %refs_3_.1) | copy-start | bytes 983044
  2.3 0.7 copy-start.7
  3.0 0.7 copy-start.8
  15.7 0.7 copy-start
  16.4 0.7 copy-start.2
  17.0 0.6 copy-start.3
  17.7 0.6 copy-start.4
  18.3 0.6 copy-start.5
  18.9 0.6 copy-start.6

commit v3 on v2

--- a/solution.py
+++ b/solution.py
@@ -20,6 +20,10 @@
     return lax.broadcasted_iota(jnp.int32, shape, dim)
 
 
+def in_hbm(array):
+    return pltpu.with_memory_space_constraint(array, pltpu.HBM)
+
+
 def x_slot(ref, seq, blocks):
     if blocks == 1:
         return ref.at[pl.ds(seq % 2, 1), seq // 2]
@@ -27,9 +31,10 @@
 
 
 def exchange_kernel(
-    shard_rows, ids_ref, routes_ref, start_ref, vision_ref, gain_ref,
+    shard_rows, ids_hbm, routes_hbm, start_ref, vision_hbm, gain_hbm,
     local_ref, pick_ref, selector_ref, image_ref, placed_ref, x_ref,
-    pack, pack_recv, x_send, x_recv, id_sems, x_sems,
+    ids_ref, routes_ref, vision_ref, gain_ref,
+    pack, pack_recv, x_send, x_recv, load_sems, id_sems, x_sems,
 ):
     n = lax.axis_size("seq")
     s, v = lax.axis_index("seq"), lax.axis_index("vocab")
@@ -39,21 +44,32 @@
     cap = selector_ref.shape[0] // n
     blocks, block, depth = x_send.shape[1:]
 
+    loads = [
+        pltpu.make_async_copy(source, target, load_sems.at[k])
+        for k, (source, target) in enumerate((
+            (vision_hbm, vision_ref), (gain_hbm, gain_ref), (ids_hbm, ids_ref), (routes_hbm, routes_ref)
+        ))
+    ]
+    for load in loads:
+        load.start()
     barrier = pltpu.get_barrier_semaphore()
     for d in range(1, n):
         pl.semaphore_signal(barrier, inc=1, **at(lax.rem(s + d, n), v))
+    for load in loads:
+        load.wait()
 
     pack[...] = jnp.full(pack.shape, -1, i32)
     pack[0:1, :tokens] = ids_ref[...]
     pack[1:2, :slots] = routes_ref[...]
     pack_recv[s] = pack[...]
 
-    group = gain_ref.shape[1]
+    group = gain_ref.shape[0]
+    gain = gain_ref[...][None, :]
     for g in range(vision_ref.shape[1] // group):
         values = vision_ref[:, g * group : (g + 1) * group].astype(f32)
         center = values - jnp.mean(values, axis=-1, keepdims=True)
         spread = jnp.mean(center * center, axis=-1, keepdims=True)
-        normed = (center / jnp.sqrt(spread + 1e-06) * gain_ref[...]).astype(bf16)
+        normed = (center / jnp.sqrt(spread + 1e-06) * gain).astype(bf16)
         for k in range(group // depth):
             part = normed[:, k * depth : (k + 1) * depth]
             for i in range(blocks):
@@ -166,6 +182,7 @@
     i32, bf16 = jnp.int32, jnp.bfloat16
     vmem = pl.BlockSpec(memory_space=pltpu.VMEM)
     smem = pl.BlockSpec(memory_space=pltpu.SMEM)
+    hbm = pl.BlockSpec(memory_space=pltpu.HBM)
     dma = pltpu.SemaphoreType.DMA
     shape = jax.ShapeDtypeStruct
     held = PAIR * min(n * id_cap, 128)
@@ -183,13 +200,18 @@
             shape((tokens, n * id_cap), bf16),
             shape((2, voc, block, depth), bf16),
         ),
-        in_specs=[vmem, vmem, smem, vmem, vmem],
+        in_specs=[hbm, hbm, smem, hbm, hbm],
         out_specs=(vmem,) * 6,
         scratch_shapes=[
+            pltpu.VMEM((1, tokens), i32),
+            pltpu.VMEM((1, slots), i32),
+            pltpu.VMEM(vision.shape, vision.dtype),
+            pltpu.VMEM(gain.shape, gain.dtype),
             pltpu.VMEM((8, LANES), i32),
             pltpu.VMEM((n, 8, LANES), i32),
             pltpu.VMEM((n, blocks, block, depth), bf16),
             pltpu.VMEM((2, voc, block, depth), bf16),
+            dma((4,)),
             dma((2, n)),
             dma((2, n)),
         ],
@@ -197,13 +219,28 @@
             collective_id=1, has_side_effects=True, vmem_limit_bytes=16 * 1024 * 1024
         ),
         name="exchange",
-    )(token_ids[None, :], routes.reshape(1, slots), splice_start, vision, gain[None, :])
-
-
-def gather_kernel(ids_ref, pick_ref, table_ref, out_ref, held, sems):
+    )(
+        in_hbm(token_ids[None, :]),
+        in_hbm(routes.reshape(1, slots)),
+        splice_start,
+        in_hbm(vision),
+        in_hbm(gain),
+    )
+
+
+def columns(width):
+    return 256 if width % 256 == 0 else width
+
+
+def gather_kernel(
+    ids_ref, pick_ref, x_ref, table_ref, w1_hbm, out_ref, sib_ref, own_ref, w1, held, sems, w_sem
+):
     groups, cap = ids_ref.shape
     span = pick_ref.shape[1]
     per = span // (PAIR * cap)
+    core = lax.axis_index("seq") % 2
+    load = pltpu.make_async_copy(w1_hbm, w1, w_sem)
+    load.start()
 
     def issue(g, carry):
         for k in range(cap):
@@ -215,6 +252,18 @@
         return carry
 
     lax.fori_loop(0, groups, issue, 0)
+
+    load.wait()
+    mid = w1.shape[1]
+    step = columns(mid)
+    theirs = x_ref[1 - core].reshape(-1, w1.shape[0])
+    ours = x_ref[core].reshape(-1, w1.shape[0])
+    for k in range(0, mid, step):
+        weight = w1[:, k : k + step]
+        sib_ref[:, k : k + step] = jnp.dot(
+            theirs, weight, preferred_element_type=jnp.float32
+        ).astype(sib_ref.dtype)
+        own_ref[:, k : k + step] = jnp.dot(ours, weight, preferred_element_type=jnp.float32)
 
     for g in range(groups // per):
         block = held.at[g * span : (g + 1) * span, :]
@@ -227,30 +276,37 @@
             out_ref[rows, k : k + 256] = found.astype(out_ref.dtype)
 
 
-def gather_rows(local_ids, pick, table):
+def gather_rows(local_ids, pick, x, table, w1):
     groups, cap = local_ids.shape
     width = table.shape[1]
-    found = pl.pallas_call(
+    rows, mid = x.shape[1] * x.shape[2], w1.shape[1]
+    vmem = pl.BlockSpec(memory_space=pltpu.VMEM)
+    hbm = pl.BlockSpec(memory_space=pltpu.HBM)
+    shape = jax.ShapeDtypeStruct
+    found, theirs, ours = pl.pallas_call(
         gather_kernel,
-        out_shape=jax.ShapeDtypeStruct((groups * cap, width), table.dtype),
-        in_specs=[
-            pl.BlockSpec(memory_space=pltpu.SMEM),
-            pl.BlockSpec(memory_space=pltpu.VMEM),
-            pl.BlockSpec(memory_space=pl.ANY),
-        ],
-        out_specs=pl.BlockSpec(memory_space=pltpu.VMEM),
+        out_shape=(
+            shape((groups * cap, width), table.dtype),
+            shape((rows, mid), jnp.bfloat16),
+            shape((rows, mid), jnp.float32),
+        ),
+        in_specs=[pl.BlockSpec(memory_space=pltpu.SMEM), vmem, vmem, hbm, hbm],
+        out_specs=(vmem,) * 3,
         scratch_shapes=[
+            pltpu.VMEM(w1.shape, w1.dtype),
             pltpu.VMEM((groups * cap * PAIR, width), table.dtype),
             pltpu.SemaphoreType.DMA((groups * cap * PAIR // pick.shape[1],)),
+            pltpu.SemaphoreType.DMA,
         ],
+        compiler_params=pltpu.CompilerParams(vmem_limit_bytes=16 * 1024 * 1024),
         name="gather_rows",
-    )(local_ids, pick, table)
-    return found.reshape(groups, cap, width)
+    )(local_ids, pick, x, table, in_hbm(w1))
+    return found.reshape(groups, cap, width), theirs, ours
 
 
 def mega_kernel(
-    x_ref, w1_hbm, w2_hbm, text_ref, selector_ref, image_ref, placed_ref, out_ref,
-    w1, w2, half_send, half_recv, half_own, plane_send, plane_recv, cross_recv,
+    half_send, half_own, w2_hbm, text_ref, selector_ref, image_ref, placed_ref, out_ref,
+    w2, half_recv, plane_send, plane_recv, cross_recv,
     h_own, h_recv, pair_send, pair_recv, pair_own, part_send, part_recv,
     row_send, row_recv, text_recv, total,
     w_sem, half_sems, plane_sems, cross_sems, h_sems,
@@ -262,13 +318,11 @@
     z, c = s // 2, s % 2
     split = n // voc
     f32, bf16 = jnp.float32, jnp.bfloat16
-    block = x_ref.shape[2]
+    block = plane_recv.shape[1]
     slots = voc * block // chips
     blocks = slots // block
 
-    load1 = pltpu.make_async_copy(w1_hbm, w1, w_sem.at[0])
-    load2 = pltpu.make_async_copy(w2_hbm, w2, w_sem.at[1])
-    load1.start()
+    load2 = pltpu.make_async_copy(w2_hbm, w2, w_sem.at[0])
     load2.start()
 
     barrier = pltpu.get_barrier_semaphore()
@@ -290,6 +344,7 @@
         copy.start()
         return copy
 
+    swap = to_peer(half_send, half_recv, half_sems, 0, s + 1 - 2 * c)
     texts = []
 
     def send_text(ds):
@@ -297,12 +352,8 @@
             peer = lax.rem(s + d, n)
             texts.append(to_peer(text_ref.at[peer], text_recv.at[s], text_sems, d, peer))
 
-    send_text(TEXT_A(n))
-    stay = pltpu.make_async_copy(text_ref.at[s], text_recv.at[s], w_sem.at[2])
-    stay.start()
-
-    def columns(width):
-        return 256 if width % 256 == 0 else width
+    send_text(text_turns(n, 0))
+    swap.wait()
 
     def chip_sums(lhs_ref, weight, to_sib, from_sib, own, sems_pair):
         width = weight.shape[1]
@@ -319,15 +370,14 @@
                 swap = to_peer(to_sib, from_sib, sems_pair, 0, s + 1 - 2 * c)
         swap.wait()
 
-    load1.wait()
-    chip_sums(x_ref, w1, half_send, half_recv, half_own, half_sems)
     copies = []
     for e in range(1, voc):
         peer = lax.rem(v + e, voc)
         span = pl.ds(pl.multiple_of(peer * block, block), block)
         plane_send[e] = (half_own[span, :] + half_recv[span, :].astype(f32)).astype(bf16)
         copies.append(to_peer(plane_send.at[e], plane_recv.at[v], plane_sems, e, s, peer))
-    send_text(TEXT_B(n))
+    text_recv[s] = text_ref[s]
+    send_text(text_turns(n, 1))
     span = pl.ds(pl.multiple_of(v * block, block), block)
     plane_recv[v] = (half_own[span, :] + half_recv[span, :].astype(f32)).astype(bf16)
     for copy in copies:
@@ -344,7 +394,7 @@
         peer = lax.rem(s + d, n)
         copies.append(to_peer(hidden_part(peer), cross_recv.at[s], cross_sems, d, peer))
     cross_recv[s] = hidden_part(s)[...]
-    send_text(TEXT_C(n))
+    send_text(text_turns(n, 2))
     for copy in copies:
         copy.wait()
     for core in range(2):
@@ -362,6 +412,7 @@
     for e in range(1, voc):
         peer = lax.rem(v + e, voc)
         copies.append(to_peer(h_own, h_place(v), h_sems, e, s, peer))
+    send_text(text_turns(n, 3))
     h_place(v)[...] = h_own[...]
     load2.wait()
     for copy in copies:
@@ -375,7 +426,7 @@
         span = pl.ds(pl.multiple_of(other * slots, slots), slots)
         part_send[d] = (pair_own[span, :] + pair_recv[span, :].astype(f32)).astype(bf16)
         sent.append(to_peer(part_send.at[d], part_recv.at[d], part_sems, d, other * 2 + c))
-    send_text(TEXT_D(n))
+    send_text(text_turns(n, 4))
     span = pl.ds(pl.multiple_of(z * slots, slots), slots)
     value = pair_own[span, :] + pair_recv[span, :].astype(f32)
     for copy in sent:
@@ -395,7 +446,6 @@
     row_recv[s] = row_send[s]
     for copy in texts:
         copy.wait()
-    stay.wait()
     step = columns(width)
     found = text_recv[...].reshape(-1, width)
     for k in range(0, width, step):
@@ -411,46 +461,35 @@
         out_ref[:, k : k + step] = value.astype(bf16)
 
 
-def TEXT_A(n):
-    return range(1, 2)
-
-
-def TEXT_B(n):
-    return range(2, n // 2)
-
-
-def TEXT_C(n):
-    return range(n // 2, 3 * n // 4)
-
-
-def TEXT_D(n):
-    return range(3 * n // 4, n)
-
-
-def mega(x, w1, w2, text, selector, image_pick, text_pick):
+CUTS = (1, 3, 5, 8, 8)
+
+
+def text_turns(n, turn):
+    order = sorted(range(1, n), key=lambda d: -min(d, n - d))
+    edges = [0] + [cut * n // 8 for cut in CUTS]
+    return order[edges[turn] : edges[turn + 1]]
+
+
+def mega(theirs, ours, w2, text, selector, image_pick, text_pick):
     n, voc = lax.axis_size("seq"), lax.axis_size("vocab")
-    block = x.shape[2]
-    slots = 2 * voc * block // n
-    rows = n // 2 * slots
+    rows, mid = theirs.shape
+    block = rows // voc
+    slots = 2 * rows // n
     blocks = slots // block
-    depth, mid = w1.shape
     inner, width = w2.shape
     cap = selector.shape[0] // n
     bf16, f32 = jnp.bfloat16, jnp.float32
     vmem = pl.BlockSpec(memory_space=pltpu.VMEM)
-    hbm = pl.BlockSpec(memory_space=pl.ANY)
+    hbm = pl.BlockSpec(memory_space=pltpu.HBM)
     dma = pltpu.SemaphoreType.DMA
     return pl.pallas_call(
         mega_kernel,
         out_shape=jax.ShapeDtypeStruct((image_pick.shape[0], width), bf16),
-        in_specs=[vmem, hbm, hbm, hbm, vmem, vmem, vmem],
+        in_specs=[vmem, vmem, hbm, vmem, vmem, vmem, vmem],
         out_specs=vmem,
         scratch_shapes=[
-            pltpu.VMEM(w1.shape, bf16),
             pltpu.VMEM(w2.shape, bf16),
-            pltpu.VMEM((voc * block, mid), bf16),
-            pltpu.VMEM((voc * block, mid), bf16),
-            pltpu.VMEM((voc * block, mid), f32),
+            pltpu.VMEM(theirs.shape, bf16),
             pltpu.VMEM((voc, block, mid), bf16),
             pltpu.VMEM((voc, block, mid), bf16),
             pltpu.VMEM((n, block, inner), bf16),
@@ -465,7 +504,7 @@
             pltpu.VMEM((n, cap, width), bf16),
             pltpu.VMEM(text.shape, bf16),
             pltpu.VMEM((image_pick.shape[0], width), f32),
-            dma((3,)),
+            dma((1,)),
             dma((2, 1)),
             dma((2, voc)),
             dma((2, n)),
@@ -476,18 +515,18 @@
             dma((2, n)),
         ],
         compiler_params=pltpu.CompilerParams(
-            collective_id=0, has_side_effects=True, vmem_limit_bytes=56 * 1024 * 1024
+            collective_id=0, has_side_effects=True, vmem_limit_bytes=24 * 1024 * 1024
         ),
         name="merger",
-    )(x, w1, w2, text, selector, image_pick, text_pick)
+    )(theirs, ours, in_hbm(w2), text, selector, image_pick, text_pick)
 
 
 def on_device(token_ids, routes, splice_start, vision, ln_gain, table, w_fc1, w_fc2):
     local_ids, pick, selector, image_pick, text_pick, x = exchange(
         token_ids, routes, splice_start, vision, ln_gain, table.shape[0], w_fc1.shape[0]
     )
-    text = gather_rows(local_ids, pick, table)
-    return mega(x, w_fc1, w_fc2, text, selector, image_pick, text_pick)
+    text, theirs, ours = gather_rows(local_ids, pick, x, table, w_fc1)
+    return mega(theirs, ours, w_fc2, text, selector, image_pick, text_pick)
 
 
 def solution(mesh):

time: 93.1 us -> 79.3 us (0.85)
  local copies, waits for them, and re-layouts: 8.64 us -> 0.8 us
  Pallas kernels: 83.8 us -> 77.8 us
    unnamed x19 -> x1, local copies, waits for them, and re-layouts: 7.94 us -> 0.8 us
    pallas_call x1, Pallas kernels: 64.4 us -> 58.2 us  [mega(): pl.pallas_call(mega_kernel, out_shape=jax.ShapeDtypeStruct((image_pick.sh...]
where the time goes in v3:
time: 79.3 us
  Pallas kernels  77.8 us (98%)
  local copies, waits for them, and re-layouts  0.8 us (1%)
    pallas_call x1, Pallas kernels, mega(): pl.pallas_call(mega_kernel, out_shape=jax.ShapeDtypeStruct((image_pick.sh...  58.2 us
    pallas_call x1, Pallas kernels, exchange(): pl.pallas_call(body, out_shape=(shape((n, id_cap), i32), shape((n * id_ca...  12.6 us
    pallas_call x1, Pallas kernels, gather_rows(): pl.pallas_call(gather_kernel, out_shape=(shape((groups * cap, width), tab...  6.98 us

profile of v3, /device:TPU:0, one launch (start us, length us, event | category | flops | bytes accessed | tf_op | source)
XLA Modules:
  0.0 79.3 jit_solution(11019994429076067436)
XLA Ops:
  0.7 12.6 %exchange.1 = (s32[8,32]{1,0:T(8,128)S(1)}, bf16[256,256]{1,0:T(8,128)(2,1)S(1)}, bf16[64,32]{1,0:T(8,128)(2,1)S(1)}, bf16[128,64]{1,0:T(8,128)(2,1)S(1)}, bf16[...) custom-call(s32[1,128]{1,0:T(1,128)} %bitcast.4, s32[1,32]{1,0:T(1,128)} %bitcast.5, s32[1]{0:T(128)S(6)} %copy.10.refs_2_, ...), custom_call_target="tpu_custom_call" | custom-call | tf_op jit(solution)/shard_map/exchange/pallas_call | solution.py:193
  13.3 7.0 %gather_rows.1 = (bf16[256,2048]{1,0:T(8,128)(2,1)S(1)}, bf16[128,1280]{1,0:T(8,128)(2,1)S(1)}, f32[128,1280]{1,0:T(8,128)S(1)}) custom-call(s32[8,32]{1,0:T(8,128)S(1)} %get-tuple-element.14.ids_ref, bf16[256,256]{1,0:T(8,128)(2,1)S(1)} %get-tuple-element.15.pick_ref, bf16[2,4,32,640]{3,2,1,0:T(8,128)(2,1)S(1)} %get-tuple-element.16.x_ref, ...), custom_call_target="tpu_custom_call" | custom-call | tf_op jit(solution)/shard_map/gather_rows/pallas_call | solution.py:286
  20.2 58.2 %merger.1 = bf16[128,2048]{1,0:T(8,128)(2,1)S(1)} custom-call(bf16[128,1280]{1,0:T(8,128)(2,1)S(1)} %get-tuple-element.17.half_send, f32[128,1280]{1,0:T(8,128)S(1)} %get-tuple-element.18.half_own, bf16[640,2048]{1,0:T(8,128)(2,1)} %w2_hbm.1, bf16[8,32,2048]{2,1,0:T(8,128)(2,1)S(1)} %bitcast.3, bf16[64,32]{1,0:T(8,128)(2,1)S(1)} %get-tuple-element.20.selector_ref, ...), custom_call_target="tpu_custom_call" | custom-call | tf_op jit(solution)/shard_map/merger/pallas_call | solution.py:485
  78.5 0.8 %copy.11 = bf16[128,2048]{1,0:T(8,128)(2,1)} copy(bf16[128,2048]{1,0:T(8,128)(2,1)S(1)} %merger.1) | data formatting | bytes 1048576

commit v4 on v3

--- a/solution.py
+++ b/solution.py
@@ -306,16 +306,17 @@
 
 def mega_kernel(
     half_send, half_own, w2_hbm, text_ref, selector_ref, image_ref, placed_ref, out_ref,
-    w2, half_recv, plane_send, plane_recv, cross_recv,
-    h_own, h_recv, pair_send, pair_recv, pair_own, part_send, part_recv,
+    w2, half_recv, plane_send, plane_recv, cross_recv, h_own, h_recv,
+    swap_send, swap_recv, chip_sum, near_send, near_recv, far_send, far_recv,
     row_send, row_recv, text_recv, total,
     w_sem, half_sems, plane_sems, cross_sems, h_sems,
-    pair_sems, part_sems, row_sems, text_sems,
+    swap_sems, near_sems, far_sems, row_sems, text_sems,
 ):
     n, voc = lax.axis_size("seq"), lax.axis_size("vocab")
     s, v = lax.axis_index("seq"), lax.axis_index("vocab")
     chips = n // 2
     z, c = s // 2, s % 2
+    pair, side = z // 2, z % 2
     split = n // voc
     f32, bf16 = jnp.float32, jnp.bfloat16
     block = plane_recv.shape[1]
@@ -330,144 +331,214 @@
         pl.semaphore_signal(barrier, inc=1, **at(lax.rem(s + d, n), v))
     for e in range(1, voc):
         pl.semaphore_signal(barrier, inc=1, **at(s, lax.rem(v + e, voc)))
-
     pl.semaphore_wait(barrier, n - 1 + voc - 1)
 
-    def to_peer(source, target, sems, d, seq, vocab=None):
+    def send(source, target, sems, spot, seq, vocab=None):
         copy = pltpu.make_async_remote_copy(
             src_ref=source,
             dst_ref=target,
-            send_sem=sems.at[0, d],
-            recv_sem=sems.at[1, d],
+            send_sem=sems.at[(0, *spot)],
+            recv_sem=sems.at[(1, *spot)],
             **at(seq, v if vocab is None else vocab),
         )
         copy.start()
         return copy
 
-    swap = to_peer(half_send, half_recv, half_sems, 0, s + 1 - 2 * c)
-    texts = []
-
-    def send_text(ds):
-        for d in ds:
-            peer = lax.rem(s + d, n)
-            texts.append(to_peer(text_ref.at[peer], text_recv.at[s], text_sems, d, peer))
-
-    send_text(text_turns(n, 0))
+    sibling = s + 1 - 2 * c
+    swap = send(half_send, half_recv, half_sems, (0,), sibling)
+
+    def text_copy(seq, source):
+        return pltpu.make_async_remote_copy(
+            src_ref=text_ref.at[seq],
+            dst_ref=text_recv.at[source],
+            send_sem=text_sems.at[0, seq],
+            recv_sem=text_sems.at[1, source],
+            **at(seq, v),
+        )
+
+    def send_text(turn):
+        for reach in range(chips - 1, -1, -1):
+            for seq in range(n):
+                for other in {seq // 2 - reach, seq // 2 + reach}:
+                    if 0 <= other < chips and text_turn(other, seq // 2, chips) == turn:
+
+                        @pl.when((z == other) & (s != seq))
+                        def _():
+                            text_copy(seq, s).start()
+
+    send_text(0)
     swap.wait()
 
-    def chip_sums(lhs_ref, weight, to_sib, from_sib, own, sems_pair):
-        width = weight.shape[1]
-        step = columns(width)
-        for core, keep in ((1 - c, False), (c, True)):
-            lhs = lhs_ref[core].reshape(-1, weight.shape[0])
-            for k in range(0, width, step):
-                part = jnp.dot(lhs, weight[:, k : k + step], preferred_element_type=f32)
-                if keep:
-                    own[:, k : k + step] = part
-                else:
-                    to_sib[:, k : k + step] = part.astype(bf16)
-            if not keep:
-                swap = to_peer(to_sib, from_sib, sems_pair, 0, s + 1 - 2 * c)
-        swap.wait()
-
-    copies = []
-    for e in range(1, voc):
+    turns = sorted(range(1, voc), key=lambda e: e % 2)
+    plane = {}
+    for e in turns:
         peer = lax.rem(v + e, voc)
         span = pl.ds(pl.multiple_of(peer * block, block), block)
         plane_send[e] = (half_own[span, :] + half_recv[span, :].astype(f32)).astype(bf16)
-        copies.append(to_peer(plane_send.at[e], plane_recv.at[v], plane_sems, e, s, peer))
-    text_recv[s] = text_ref[s]
-    send_text(text_turns(n, 1))
+        plane[e] = send(plane_send.at[e], plane_recv.at[v], plane_sems, (e,), s, peer)
     span = pl.ds(pl.multiple_of(v * block, block), block)
     plane_recv[v] = (half_own[span, :] + half_recv[span, :].astype(f32)).astype(bf16)
-    for copy in copies:
-        copy.wait()
 
     inner = h_own.shape[2]
 
     def hidden_part(seq):
-        side = pl.multiple_of(seq % split * inner, inner) if split > 1 else 0
-        return plane_recv.at[seq // split, :, pl.ds(side, inner)]
+        where = pl.multiple_of(seq % split * inner, inner) if split > 1 else 0
+        return plane_recv.at[seq // split, :, pl.ds(where, inner)]
+
+    def cross_copy(seq):
+        return pltpu.make_async_remote_copy(
+            src_ref=hidden_part(seq),
+            dst_ref=cross_recv.at[s],
+            send_sem=cross_sems.at[0, seq],
+            recv_sem=cross_sems.at[1, s],
+            **at(seq, v),
+        )
+
+    for e in [0] + turns:
+        if e:
+            plane[e].wait()
+        source = lax.rem(v + voc - e, voc)
+        for j in range(split):
+            seq = source * split + j
+
+            @pl.when(seq != s)
+            def _():
+                cross_copy(seq).start()
+
+            @pl.when(seq == s)
+            def _():
+                cross_recv[s] = hidden_part(seq)[...]
+
+        if e == 0:
+            text_recv[s] = text_ref[s]
+            send_text(1)
+    send_text(2)
+
+    def h_place(core, vocab):
+        if blocks == 1:
+            return h_recv.at[core, vocab, 0]
+        return h_recv.at[vocab % 2, vocab // 2, core]
 
     copies = []
-    for d in range(1, n):
-        peer = lax.rem(s + d, n)
-        copies.append(to_peer(hidden_part(peer), cross_recv.at[s], cross_sems, d, peer))
-    cross_recv[s] = hidden_part(s)[...]
-    send_text(text_turns(n, 2))
-    for copy in copies:
-        copy.wait()
     for core in range(2):
+        for k in range(chips):
+            r = 2 * k + core
+
+            @pl.when(r != s)
+            def _():
+                pltpu.make_async_remote_copy(
+                    src_ref=cross_recv.at[r],
+                    dst_ref=cross_recv.at[r],
+                    send_sem=cross_sems.at[0, r],
+                    recv_sem=cross_sems.at[1, r],
+                    **at(sibling, v),
+                ).wait_recv()
+
         pre = cross_recv[core].astype(f32)
         for k in range(1, chips):
             pre = pre + cross_recv[2 * k + core].astype(f32)
         h_own[core] = (0.5 * pre * (1.0 + lax.erf(pre * math.sqrt(0.5)))).astype(bf16)
-
-    def h_place(vocab):
-        if blocks == 1:
-            return h_recv.at[:, vocab, 0]
-        return h_recv.at[vocab % 2, vocab // 2]
-
-    copies = []
-    for e in range(1, voc):
-        peer = lax.rem(v + e, voc)
-        copies.append(to_peer(h_own, h_place(v), h_sems, e, s, peer))
-    send_text(text_turns(n, 3))
-    h_place(v)[...] = h_own[...]
+        for e in turns:
+            peer = lax.rem(v + e, voc)
+            copies.append(send(h_own.at[core], h_place(core, v), h_sems, (core, e), s, peer))
+        h_place(core, v)[...] = h_own[core]
+    send_text(3)
     load2.wait()
     for copy in copies:
         copy.wait()
 
     width = w2.shape[1]
-    chip_sums(h_recv, w2, pair_send, pair_recv, pair_own, pair_sems)
-    sent = []
-    for d in range(1, chips):
-        other = lax.rem(z + d, chips)
-        span = pl.ds(pl.multiple_of(other * slots, slots), slots)
-        part_send[d] = (pair_own[span, :] + pair_recv[span, :].astype(f32)).astype(bf16)
-        sent.append(to_peer(part_send.at[d], part_recv.at[d], part_sems, d, other * 2 + c))
-    send_text(text_turns(n, 4))
-    span = pl.ds(pl.multiple_of(z * slots, slots), slots)
-    value = pair_own[span, :] + pair_recv[span, :].astype(f32)
-    for copy in sent:
-        copy.wait()
-    for d in range(1, chips):
-        value = value + part_recv[d].astype(f32)
-    merged = value.astype(bf16)
-
+    step = 512 if width % 512 == 0 else width
+    chunks = [slice(k, k + step) for k in range(0, width, step)]
+    depth = w2.shape[0]
+    theirs = h_recv[1 - c].reshape(-1, depth)
+    ours = h_recv[c].reshape(-1, depth)
+    swaps = []
+    for k, cols in enumerate(chunks):
+        part = jnp.dot(theirs, w2[:, cols], preferred_element_type=f32)
+        swap_send[:, cols] = part.astype(bf16)
+        swaps.append(send(swap_send.at[:, cols], swap_recv.at[:, cols], swap_sems, (k,), sibling))
+    nears = []
+    for k, cols in enumerate(chunks):
+        part = jnp.dot(ours, w2[:, cols], preferred_element_type=f32)
+        swaps[k].wait()
+        part = part + swap_recv[:, cols].astype(f32)
+        chip_sum[:, :, :, cols] = part.reshape(chips // 2, 2, slots, step)
+        for i in range(chips // 2):
+            near_send[i, :, cols] = chip_sum[i, 1 - side, :, cols].astype(bf16)
+        nears.append(send(
+            near_send.at[:, :, cols], near_recv.at[:, :, cols], near_sems, (k,), s + 2 - 4 * side
+        ))
+    send_text(4)
+    fars = []
+    for k, cols in enumerate(chunks):
+        nears[k].wait()
+        row = []
+        for i in range(1, chips // 2):
+            other = lax.rem(pair + i, chips // 2)
+            value = chip_sum[other, side, :, cols] + near_recv[other, :, cols].astype(f32)
+            far_send[i, :, cols] = value.astype(bf16)
+            row.append(send(
+                far_send.at[i, :, cols], far_recv.at[i, :, cols], far_sems, (k, i),
+                4 * other + 2 * side + c,
+            ))
+        fars.append(row)
     cap = row_send.shape[1]
-    outgoing = jnp.dot(selector_ref[...], merged, preferred_element_type=f32).astype(bf16)
-    for t in range(n):
-        row_send[t] = outgoing[t * cap : (t + 1) * cap]
     copies = []
-    for d in range(1, n):
-        peer = lax.rem(s + d, n)
-        copies.append(to_peer(row_send.at[peer], row_recv.at[s], row_sems, d, peer))
-    row_recv[s] = row_send[s]
-    for copy in texts:
-        copy.wait()
-    step = columns(width)
+    for k, cols in enumerate(chunks):
+        value = chip_sum[pair, side, :, cols] + near_recv[pair, :, cols].astype(f32)
+        for i, copy in enumerate(fars[k]):
+            copy.wait()
+            value = value + far_recv[i + 1, :, cols].astype(f32)
+        merged = value.astype(bf16)
+        outgoing = jnp.dot(selector_ref[...], merged, preferred_element_type=f32).astype(bf16)
+        for t in range(n):
+            row_send[t, :, cols] = outgoing[t * cap : (t + 1) * cap]
+        row = []
+        for d in range(1, n):
+            peer = lax.rem(s + d, n)
+            row.append(send(
+                row_send.at[peer, :, cols], row_recv.at[s, :, cols], row_sems, (k, d), peer
+            ))
+        row_recv[s, :, cols] = row_send[s, :, cols]
+        copies.append(row)
+    for seq in range(n):
+
+        @pl.when(seq != s)
+        def _():
+            text_copy(seq, s).wait_send()
+            text_copy(s, seq).wait_recv()
+
     found = text_recv[...].reshape(-1, width)
-    for k in range(0, width, step):
-        total[:, k : k + step] = jnp.dot(
-            placed_ref[...], found[:, k : k + step], preferred_element_type=f32
+    for cols in chunks:
+        total[:, cols] = jnp.dot(
+            placed_ref[...], found[:, cols], preferred_element_type=f32
         )
-    for copy in copies:
-        copy.wait()
-    for k in range(0, width, step):
-        value = total[:, k : k + step]
-        block_rows = row_recv[:, :, k : k + step].astype(f32).reshape(n * cap, step).astype(bf16)
-        value = value + jnp.dot(image_ref[...], block_rows, preferred_element_type=f32)
-        out_ref[:, k : k + step] = value.astype(bf16)
-
-
-CUTS = (1, 3, 5, 8, 8)
-
-
-def text_turns(n, turn):
-    order = sorted(range(1, n), key=lambda d: -min(d, n - d))
-    edges = [0] + [cut * n // 8 for cut in CUTS]
-    return order[edges[turn] : edges[turn + 1]]
+    for k, cols in enumerate(chunks):
+        for copy in copies[k]:
+            copy.wait()
+        rows = row_recv[:, :, cols].astype(f32).reshape(n * cap, step).astype(bf16)
+        value = total[:, cols] + jnp.dot(image_ref[...], rows, preferred_element_type=f32)
+        out_ref[:, cols] = value.astype(bf16)
+    for r in range(n):
+        @pl.when(r != s)
+        def _():
+            cross_copy(r).wait_send()
+
+
+TURNS = (0, 0, 2, 2, 3, 2)
+
+
+def text_turn(source, target, chips):
+    reach = abs(source - target)
+    outer = source in (0, chips - 1)
+    if reach == 0:
+        return TURNS[5]
+    if reach > chips // 2:
+        return TURNS[0]
+    if reach > chips // 4:
+        return TURNS[1] if outer else TURNS[2]
+    return TURNS[3] if outer or target in (0, chips - 1) else TURNS[4]
 
 
 def mega(theirs, ours, w2, text, selector, image_pick, text_pick):
@@ -477,6 +548,7 @@
     slots = 2 * rows // n
     blocks = slots // block
     inner, width = w2.shape
+    chunks = width // 512 if width % 512 == 0 else 1
     cap = selector.shape[0] // n
     bf16, f32 = jnp.bfloat16, jnp.float32
     vmem = pl.BlockSpec(memory_space=pltpu.VMEM)
@@ -497,9 +569,11 @@
             pltpu.VMEM((2, n // 2, blocks, block, inner), bf16),
             pltpu.VMEM((rows, width), bf16),
             pltpu.VMEM((rows, width), bf16),
-            pltpu.VMEM((rows, width), f32),
-            pltpu.VMEM((n // 2, slots, width), bf16),
-            pltpu.VMEM((n // 2, slots, width), bf16),
+            pltpu.VMEM((n // 4, 2, slots, width), f32),
+            pltpu.VMEM((n // 4, slots, width), bf16),
+            pltpu.VMEM((n // 4, slots, width), bf16),
+            pltpu.VMEM((n // 4, slots, width), bf16),
+            pltpu.VMEM((n // 4, slots, width), bf16),
             pltpu.VMEM((n, cap, width), bf16),
             pltpu.VMEM((n, cap, width), bf16),
             pltpu.VMEM(text.shape, bf16),
@@ -508,10 +582,11 @@
             dma((2, 1)),
             dma((2, voc)),
             dma((2, n)),
-            dma((2, voc)),
-            dma((2, 1)),
-            dma((2, n // 2)),
-            dma((2, n)),
+            dma((2, 2, voc)),
+            dma((2, chunks)),
+            dma((2, chunks)),
+            dma((2, chunks, n // 4)),
+            dma((2, chunks, n)),
             dma((2, n)),
         ],
         compiler_params=pltpu.CompilerParams(

time: 79.3 us -> 74.1 us (0.934)
  Pallas kernels: 77.8 us -> 72.4 us
    pallas_call x1, Pallas kernels: 58.2 us -> 52.7 us  [mega(): pl.pallas_call(mega_kernel, out_shape=jax.ShapeDtypeStruct((image_pick.sh...]
where the time goes in v4:
time: 74.1 us; the launch traced here: 73.9 us
  Pallas kernels  72.4 us (98%)
  local copies, waits for them, and re-layouts  0.8 us (1%)
    pallas_call x1, Pallas kernels, mega(): pl.pallas_call(mega_kernel, out_shape=jax.ShapeDtypeStruct((image_pick.sh...  52.7 us
    pallas_call x1, Pallas kernels, exchange(): pl.pallas_call(body, out_shape=(shape((n, id_cap), i32), shape((n * id_ca...  12.6 us
    pallas_call x1, Pallas kernels, gather_rows(): pl.pallas_call(gather_kernel, out_shape=(shape((groups * cap, width), tab...  7.11 us

profile of v4, /device:TPU:0, one launch (start us, length us, event | category | flops | bytes accessed | tf_op | source)
XLA Modules:
  0.0 73.9 jit_solution(18430782396684671902)
XLA Ops:
  0.7 12.6 %exchange.1 = (s32[8,32]{1,0:T(8,128)S(1)}, bf16[256,256]{1,0:T(8,128)(2,1)S(1)}, bf16[64,32]{1,0:T(8,128)(2,1)S(1)}, bf16[128,64]{1,0:T(8,128)(2,1)S(1)}, bf16[...) custom-call(s32[1,128]{1,0:T(1,128)} %bitcast.4, s32[1,32]{1,0:T(1,128)} %bitcast.5, s32[1]{0:T(128)S(6)} %copy.10.refs_2_, ...), custom_call_target="tpu_custom_call" | custom-call | tf_op jit(solution)/shard_map/exchange/pallas_call | solution.py:193
  13.3 7.1 %gather_rows.1 = (bf16[256,2048]{1,0:T(8,128)(2,1)S(1)}, bf16[128,1280]{1,0:T(8,128)(2,1)S(1)}, f32[128,1280]{1,0:T(8,128)S(1)}) custom-call(s32[8,32]{1,0:T(8,128)S(1)} %get-tuple-element.14.ids_ref, bf16[256,256]{1,0:T(8,128)(2,1)S(1)} %get-tuple-element.15.pick_ref, bf16[2,4,32,640]{3,2,1,0:T(8,128)(2,1)S(1)} %get-tuple-element.16.x_ref, ...), custom_call_target="tpu_custom_call" | custom-call | tf_op jit(solution)/shard_map/gather_rows/pallas_call | solution.py:286
  20.4 52.7 %merger.1 = bf16[128,2048]{1,0:T(8,128)(2,1)S(1)} custom-call(bf16[128,1280]{1,0:T(8,128)(2,1)S(1)} %get-tuple-element.17.half_send, f32[128,1280]{1,0:T(8,128)S(1)} %get-tuple-element.18.half_own, bf16[640,2048]{1,0:T(8,128)(2,1)} %w2_hbm.1, bf16[8,32,2048]{2,1,0:T(8,128)(2,1)S(1)} %bitcast.3, bf16[64,32]{1,0:T(8,128)(2,1)S(1)} %get-tuple-element.20.selector_ref, ...), custom_call_target="tpu_custom_call" | custom-call | tf_op jit(solution)/shard_map/merger/pallas_call | solution.py:557
  73.1 0.8 %copy.11 = bf16[128,2048]{1,0:T(8,128)(2,1)} copy(bf16[128,2048]{1,0:T(8,128)(2,1)S(1)} %merger.1) | data formatting | bytes 1048576

commit v5 on v4

--- a/solution.py
+++ b/solution.py
@@ -24,17 +24,11 @@
     return pltpu.with_memory_space_constraint(array, pltpu.HBM)
 
 
-def x_slot(ref, seq, blocks):
-    if blocks == 1:
-        return ref.at[pl.ds(seq % 2, 1), seq // 2]
-    return ref.at[:, seq]
-
-
 def exchange_kernel(
-    shard_rows, ids_hbm, routes_hbm, start_ref, vision_hbm, gain_hbm,
-    local_ref, pick_ref, selector_ref, image_ref, placed_ref, x_ref,
+    shard_rows, ids_hbm, routes_hbm, start_ref, vision_hbm, gain_hbm, w1_hbm,
+    local_ref, pick_ref, selector_ref, image_ref, placed_ref, x_ref, w1_ref,
     ids_ref, routes_ref, vision_ref, gain_ref,
-    pack, pack_recv, x_send, x_recv, load_sems, id_sems, x_sems,
+    pack, pack_recv, x_send, x_recv, load_sems, id_sems, x_sems, w_sems,
 ):
     n = lax.axis_size("seq")
     s, v = lax.axis_index("seq"), lax.axis_index("vocab")
@@ -43,11 +37,13 @@
     id_cap = local_ref.shape[1]
     cap = selector_ref.shape[0] // n
     blocks, block, depth = x_send.shape[1:]
+    z, c = s // 2, s % 2
 
     loads = [
         pltpu.make_async_copy(source, target, load_sems.at[k])
         for k, (source, target) in enumerate((
-            (vision_hbm, vision_ref), (gain_hbm, gain_ref), (ids_hbm, ids_ref), (routes_hbm, routes_ref)
+            (vision_hbm, vision_ref), (gain_hbm, gain_ref), (ids_hbm, ids_ref), (routes_hbm, routes_ref),
+            (w1_hbm, w1_ref.at[c]),
         ))
     ]
     for load in loads:
@@ -55,7 +51,7 @@
     barrier = pltpu.get_barrier_semaphore()
     for d in range(1, n):
         pl.semaphore_signal(barrier, inc=1, **at(lax.rem(s + d, n), v))
-    for load in loads:
+    for load in loads[:4]:
         load.wait()
 
     pack[...] = jnp.full(pack.shape, -1, i32)
@@ -92,12 +88,21 @@
     for d in range(1, n):
         peer = lax.rem(s + d, n)
         id_copies.append(to_peer(pack, pack_recv.at[s], id_sems, d, peer))
-    for d in range(1, n):
-        peer = lax.rem(s + d, n)
-        x_copies.append(
-            to_peer(x_send.at[peer], x_slot(x_recv, s, blocks), x_sems, d, peer)
-        )
-    x_slot(x_recv, s, blocks)[...] = x_send[s]
+    if blocks == 1:
+        for d in range(1, n // 2):
+            other = lax.rem(z + d, n // 2)
+            x_copies.append(
+                to_peer(x_send.at[other, 0], x_recv.at[z], x_sems, d, 2 * other + c)
+            )
+        x_recv[z] = x_send[z, 0]
+    else:
+        for d in range(1, n):
+            peer = lax.rem(s + d, n)
+            x_copies.append(
+                to_peer(x_send.at[peer // 2, peer % 2], x_recv.at[s], x_sems, d, peer)
+            )
+        x_recv[s] = x_send[z, c]
+    share = to_peer(w1_hbm, w1_ref.at[c], w_sems, 0, s + 1 - 2 * c)
 
     lane_t = iota((tokens, tokens), 1)
     upto = (iota((tokens, tokens), 0) <= lane_t).astype(bf16)
@@ -171,13 +176,16 @@
     for copy in x_copies:
         copy.wait()
     x_ref[...] = x_recv[...]
-
-
-def exchange(token_ids, routes, splice_start, vision, gain, table_rows, depth):
+    loads[4].wait()
+    share.wait()
+
+
+def exchange(token_ids, routes, splice_start, vision, gain, table_rows, w1):
     n, voc = lax.axis_size("seq"), lax.axis_size("vocab")
     tokens, slots = token_ids.shape[0], routes.shape[0]
     block = n * slots // (2 * voc)
     blocks = slots // block
+    depth = 2 * w1.shape[0]
     id_cap, cap = 2 * tokens // n, 2 * slots // n
     i32, bf16 = jnp.int32, jnp.bfloat16
     vmem = pl.BlockSpec(memory_space=pltpu.VMEM)
@@ -198,10 +206,11 @@
             shape((n * cap, slots), bf16),
             shape((tokens, n * cap), bf16),
             shape((tokens, n * id_cap), bf16),
-            shape((2, voc, block, depth), bf16),
+            shape((voc, block, depth), bf16),
+            shape((2, *w1.shape), bf16),
         ),
-        in_specs=[hbm, hbm, smem, hbm, hbm],
-        out_specs=(vmem,) * 6,
+        in_specs=[hbm, hbm, smem, hbm, hbm, hbm],
+        out_specs=(vmem,) * 7,
         scratch_shapes=[
             pltpu.VMEM((1, tokens), i32),
             pltpu.VMEM((1, slots), i32),
@@ -209,11 +218,12 @@
             pltpu.VMEM(gain.shape, gain.dtype),
             pltpu.VMEM((8, LANES), i32),
             pltpu.VMEM((n, 8, LANES), i32),
-            pltpu.VMEM((n, blocks, block, depth), bf16),
-            pltpu.VMEM((2, voc, block, depth), bf16),
-            dma((4,)),
+            pltpu.VMEM((n // 2, blocks, block, depth), bf16),
+            pltpu.VMEM((voc, block, depth), bf16),
+            dma((5,)),
             dma((2, n)),
             dma((2, n)),
+            dma((2, 1)),
         ],
         compiler_params=pltpu.CompilerParams(
             collective_id=1, has_side_effects=True, vmem_limit_bytes=16 * 1024 * 1024
@@ -225,6 +235,7 @@
         splice_start,
         in_hbm(vision),
         in_hbm(gain),
+        in_hbm(w1),
     )
 
 
@@ -233,14 +244,11 @@
 
 
 def gather_kernel(
-    ids_ref, pick_ref, x_ref, table_ref, w1_hbm, out_ref, sib_ref, own_ref, w1, held, sems, w_sem
+    ids_ref, pick_ref, x_ref, table_ref, w1_ref, out_ref, sum_ref, held, sems
 ):
     groups, cap = ids_ref.shape
     span = pick_ref.shape[1]
     per = span // (PAIR * cap)
-    core = lax.axis_index("seq") % 2
-    load = pltpu.make_async_copy(w1_hbm, w1, w_sem)
-    load.start()
 
     def issue(g, carry):
         for k in range(cap):
@@ -253,17 +261,14 @@
 
     lax.fori_loop(0, groups, issue, 0)
 
-    load.wait()
-    mid = w1.shape[1]
+    mid = w1_ref.shape[2]
     step = columns(mid)
-    theirs = x_ref[1 - core].reshape(-1, w1.shape[0])
-    ours = x_ref[core].reshape(-1, w1.shape[0])
+    voc, block, depth = x_ref.shape
+    ours = x_ref[...].reshape(voc * block, depth)
     for k in range(0, mid, step):
-        weight = w1[:, k : k + step]
-        sib_ref[:, k : k + step] = jnp.dot(
-            theirs, weight, preferred_element_type=jnp.float32
-        ).astype(sib_ref.dtype)
-        own_ref[:, k : k + step] = jnp.dot(ours, weight, preferred_element_type=jnp.float32)
+        weight = w1_ref[:, :, k : k + step].reshape(depth, step)
+        part = jnp.dot(ours, weight, preferred_element_type=jnp.float32)
+        sum_ref[:, :, k : k + step] = part.astype(sum_ref.dtype).reshape(voc, block, step)
 
     for g in range(groups // per):
         block = held.at[g * span : (g + 1) * span, :]
@@ -279,51 +284,46 @@
 def gather_rows(local_ids, pick, x, table, w1):
     groups, cap = local_ids.shape
     width = table.shape[1]
-    rows, mid = x.shape[1] * x.shape[2], w1.shape[1]
     vmem = pl.BlockSpec(memory_space=pltpu.VMEM)
     hbm = pl.BlockSpec(memory_space=pltpu.HBM)
     shape = jax.ShapeDtypeStruct
-    found, theirs, ours = pl.pallas_call(
+    found, sums = pl.pallas_call(
         gather_kernel,
         out_shape=(
             shape((groups * cap, width), table.dtype),
-            shape((rows, mid), jnp.bfloat16),
-            shape((rows, mid), jnp.float32),
+            shape((*x.shape[:2], w1.shape[2]), jnp.bfloat16),
         ),
-        in_specs=[pl.BlockSpec(memory_space=pltpu.SMEM), vmem, vmem, hbm, hbm],
-        out_specs=(vmem,) * 3,
+        in_specs=[pl.BlockSpec(memory_space=pltpu.SMEM), vmem, vmem, hbm, vmem],
+        out_specs=(vmem,) * 2,
         scratch_shapes=[
-            pltpu.VMEM(w1.shape, w1.dtype),
             pltpu.VMEM((groups * cap * PAIR, width), table.dtype),
             pltpu.SemaphoreType.DMA((groups * cap * PAIR // pick.shape[1],)),
-            pltpu.SemaphoreType.DMA,
         ],
         compiler_params=pltpu.CompilerParams(vmem_limit_bytes=16 * 1024 * 1024),
         name="gather_rows",
-    )(local_ids, pick, x, table, in_hbm(w1))
-    return found.reshape(groups, cap, width), theirs, ours
+    )(local_ids, pick, x, table, w1)
+    return found.reshape(groups, cap, width), sums
 
 
 def mega_kernel(
-    half_send, half_own, w2_hbm, text_ref, selector_ref, image_ref, placed_ref, out_ref,
-    w2, half_recv, plane_send, plane_recv, cross_recv, h_own, h_recv,
-    swap_send, swap_recv, chip_sum, near_send, near_recv, far_send, far_recv,
+    sum_ref, w2_hbm, text_ref, selector_ref, image_ref, placed_ref, out_ref,
+    w2, plane_recv, cross_recv, h_own, h_recv, halves, half_send, half_recv, chip_sum, near_send, near_recv, far_send, far_recv,
     row_send, row_recv, text_recv, total,
-    w_sem, half_sems, plane_sems, cross_sems, h_sems,
-    swap_sems, near_sems, far_sems, row_sems, text_sems,
+    w_sem, share_sems, plane_sems, cross_sems, h_sems,
+    half_sems, near_sems, far_sems, row_sems, text_sems,
 ):
     n, voc = lax.axis_size("seq"), lax.axis_size("vocab")
     s, v = lax.axis_index("seq"), lax.axis_index("vocab")
     chips = n // 2
     z, c = s // 2, s % 2
     pair, side = z // 2, z % 2
-    split = n // voc
+    per = voc // chips
     f32, bf16 = jnp.float32, jnp.bfloat16
     block = plane_recv.shape[1]
     slots = voc * block // chips
     blocks = slots // block
 
-    load2 = pltpu.make_async_copy(w2_hbm, w2, w_sem.at[0])
+    load2 = pltpu.make_async_copy(w2_hbm, w2.at[c], w_sem.at[0])
     load2.start()
 
     barrier = pltpu.get_barrier_semaphore()
@@ -345,7 +345,11 @@
         return copy
 
     sibling = s + 1 - 2 * c
-    swap = send(half_send, half_recv, half_sems, (0,), sibling)
+    turns = sorted(range(1, voc), key=lambda e: e % 2)
+    plane = {}
+    for e in turns:
+        peer = lax.rem(v + e, voc)
+        plane[e] = send(sum_ref.at[peer], plane_recv.at[v], plane_sems, (e,), s, peer)
 
     def text_copy(seq, source):
         return pltpu.make_async_remote_copy(
@@ -367,102 +371,77 @@
                             text_copy(seq, s).start()
 
     send_text(0)
-    swap.wait()
-
-    turns = sorted(range(1, voc), key=lambda e: e % 2)
-    plane = {}
-    for e in turns:
-        peer = lax.rem(v + e, voc)
-        span = pl.ds(pl.multiple_of(peer * block, block), block)
-        plane_send[e] = (half_own[span, :] + half_recv[span, :].astype(f32)).astype(bf16)
-        plane[e] = send(plane_send.at[e], plane_recv.at[v], plane_sems, (e,), s, peer)
-    span = pl.ds(pl.multiple_of(v * block, block), block)
-    plane_recv[v] = (half_own[span, :] + half_recv[span, :].astype(f32)).astype(bf16)
-
-    inner = h_own.shape[2]
-
-    def hidden_part(seq):
-        where = pl.multiple_of(seq % split * inner, inner) if split > 1 else 0
-        return plane_recv.at[seq // split, :, pl.ds(where, inner)]
-
-    def cross_copy(seq):
+    share = send(w2_hbm, w2.at[c], share_sems, (0,), sibling)
+    plane_recv[v] = sum_ref[v]
+
+    def cross_copy(column):
+        place = lax.rem(column, per)
         return pltpu.make_async_remote_copy(
-            src_ref=hidden_part(seq),
-            dst_ref=cross_recv.at[s],
-            send_sem=cross_sems.at[0, seq],
-            recv_sem=cross_sems.at[1, s],
-            **at(seq, v),
+            src_ref=plane_recv.at[column],
+            dst_ref=cross_recv.at[z, place],
+            send_sem=cross_sems.at[0, column],
+            recv_sem=cross_sems.at[1, z * per + place],
+            **at(2 * (column // per) + c, v),
         )
 
     for e in [0] + turns:
         if e:
             plane[e].wait()
-        source = lax.rem(v + voc - e, voc)
-        for j in range(split):
-            seq = source * split + j
-
-            @pl.when(seq != s)
-            def _():
-                cross_copy(seq).start()
-
-            @pl.when(seq == s)
-            def _():
-                cross_recv[s] = hidden_part(seq)[...]
+        column = lax.rem(v + voc - e, voc)
+
+        @pl.when(column // per != z)
+        def _():
+            cross_copy(column).start()
+
+        @pl.when(column // per == z)
+        def _():
+            cross_recv[z, lax.rem(column, per)] = plane_recv[column]
 
         if e == 0:
             text_recv[s] = text_ref[s]
             send_text(1)
     send_text(2)
 
-    def h_place(core, vocab):
-        if blocks == 1:
-            return h_recv.at[core, vocab, 0]
-        return h_recv.at[vocab % 2, vocab // 2, core]
-
-    copies = []
-    for core in range(2):
-        for k in range(chips):
-            r = 2 * k + core
-
-            @pl.when(r != s)
-            def _():
+    mid = plane_recv.shape[2]
+    for k in range(chips):
+
+        @pl.when(k != z)
+        def _():
+            for i in range(per):
                 pltpu.make_async_remote_copy(
-                    src_ref=cross_recv.at[r],
-                    dst_ref=cross_recv.at[r],
-                    send_sem=cross_sems.at[0, r],
-                    recv_sem=cross_sems.at[1, r],
+                    src_ref=cross_recv.at[k, i],
+                    dst_ref=cross_recv.at[k, i],
+                    send_sem=cross_sems.at[0, k * per + i],
+                    recv_sem=cross_sems.at[1, k * per + i],
                     **at(sibling, v),
                 ).wait_recv()
 
-        pre = cross_recv[core].astype(f32)
+    for i in range(per):
+        pre = cross_recv[0, i].astype(f32)
         for k in range(1, chips):
-            pre = pre + cross_recv[2 * k + core].astype(f32)
-        h_own[core] = (0.5 * pre * (1.0 + lax.erf(pre * math.sqrt(0.5)))).astype(bf16)
-        for e in turns:
-            peer = lax.rem(v + e, voc)
-            copies.append(send(h_own.at[core], h_place(core, v), h_sems, (core, e), s, peer))
-        h_place(core, v)[...] = h_own[core]
+            pre = pre + cross_recv[k, i].astype(f32)
+        h_own[:, i * mid : (i + 1) * mid] = (
+            0.5 * pre * (1.0 + lax.erf(pre * math.sqrt(0.5)))
+        ).astype(bf16)
+    copies = []
+    for e in turns:
+        peer = lax.rem(v + e, voc)
+        copies.append(send(h_own, h_recv.at[v], h_sems, (e,), s, peer))
+    h_recv[v] = h_own[...]
     send_text(3)
     load2.wait()
+    share.wait()
     for copy in copies:
         copy.wait()
 
-    width = w2.shape[1]
+    width = w2.shape[2]
     step = 512 if width % 512 == 0 else width
     chunks = [slice(k, k + step) for k in range(0, width, step)]
-    depth = w2.shape[0]
-    theirs = h_recv[1 - c].reshape(-1, depth)
-    ours = h_recv[c].reshape(-1, depth)
-    swaps = []
-    for k, cols in enumerate(chunks):
-        part = jnp.dot(theirs, w2[:, cols], preferred_element_type=f32)
-        swap_send[:, cols] = part.astype(bf16)
-        swaps.append(send(swap_send.at[:, cols], swap_recv.at[:, cols], swap_sems, (k,), sibling))
+    hidden = h_recv[...].reshape(voc * block, h_recv.shape[2])
     nears = []
     for k, cols in enumerate(chunks):
-        part = jnp.dot(ours, w2[:, cols], preferred_element_type=f32)
-        swaps[k].wait()
-        part = part + swap_recv[:, cols].astype(f32)
+        weight = w2[:, :, cols].reshape(h_recv.shape[2], step)
+        part = jnp.dot(hidden, weight, preferred_element_type=f32)
         chip_sum[:, :, :, cols] = part.reshape(chips // 2, 2, slots, step)
         for i in range(chips // 2):
             near_send[i, :, cols] = chip_sum[i, 1 - side, :, cols].astype(bf16)
@@ -491,6 +470,14 @@
             copy.wait()
             value = value + far_recv[i + 1, :, cols].astype(f32)
         merged = value.astype(bf16)
+        if blocks == 2:
+            halves[:, :, cols] = merged.reshape(2, block, step)
+            half_send[:, cols] = halves[1 - c, :, cols]
+            send(
+                half_send.at[:, cols], half_recv.at[:, cols], half_sems, (k,), sibling
+            ).wait()
+            halves[1 - c, :, cols] = half_recv[:, cols]
+            merged = halves[:, :, cols].reshape(slots, step)
         outgoing = jnp.dot(selector_ref[...], merged, preferred_element_type=f32).astype(bf16)
         for t in range(n):
             row_send[t, :, cols] = outgoing[t * cap : (t + 1) * cap]
@@ -520,10 +507,11 @@
         rows = row_recv[:, :, cols].astype(f32).reshape(n * cap, step).astype(bf16)
         value = total[:, cols] + jnp.dot(image_ref[...], rows, preferred_element_type=f32)
         out_ref[:, cols] = value.astype(bf16)
-    for r in range(n):
-        @pl.when(r != s)
+    for column in range(voc):
+
+        @pl.when(column // per != z)
         def _():
-            cross_copy(r).wait_send()
+            cross_copy(column).wait_send()
 
 
 TURNS = (0, 0, 2, 2, 3, 2)
@@ -541,11 +529,10 @@
     return TURNS[3] if outer or target in (0, chips - 1) else TURNS[4]
 
 
-def mega(theirs, ours, w2, text, selector, image_pick, text_pick):
+def mega(sums, w2, text, selector, image_pick, text_pick):
     n, voc = lax.axis_size("seq"), lax.axis_size("vocab")
-    rows, mid = theirs.shape
-    block = rows // voc
-    slots = 2 * rows // n
+    block, mid = sums.shape[1:]
+    slots = 2 * voc * block // n
     blocks = slots // block
     inner, width = w2.shape
     chunks = width // 512 if width % 512 == 0 else 1
@@ -557,18 +544,17 @@
     return pl.pallas_call(
         mega_kernel,
         out_shape=jax.ShapeDtypeStruct((image_pick.shape[0], width), bf16),
-        in_specs=[vmem, vmem, hbm, vmem, vmem, vmem, vmem],
+        in_specs=[vmem, hbm, vmem, vmem, vmem, vmem],
         out_specs=vmem,
         scratch_shapes=[
-            pltpu.VMEM(w2.shape, bf16),
-            pltpu.VMEM(theirs.shape, bf16),
+            pltpu.VMEM((2, *w2.shape), bf16),
             pltpu.VMEM((voc, block, mid), bf16),
-            pltpu.VMEM((voc, block, mid), bf16),
-            pltpu.VMEM((n, block, inner), bf16),
-            pltpu.VMEM((2, block, inner), bf16),
-            pltpu.VMEM((2, n // 2, blocks, block, inner), bf16),
-            pltpu.VMEM((rows, width), bf16),
-            pltpu.VMEM((rows, width), bf16),
+            pltpu.VMEM((n // 2, 2 * voc // n, block, mid), bf16),
+            pltpu.VMEM((block, 2 * inner), bf16),
+            pltpu.VMEM((voc, block, 2 * inner), bf16),
+            pltpu.VMEM((2, slots // 2, width), bf16),
+            pltpu.VMEM((slots // 2, width), bf16),
+            pltpu.VMEM((slots // 2, width), bf16),
             pltpu.VMEM((n // 4, 2, slots, width), f32),
             pltpu.VMEM((n // 4, slots, width), bf16),
             pltpu.VMEM((n // 4, slots, width), bf16),
@@ -581,8 +567,8 @@
             dma((1,)),
             dma((2, 1)),
             dma((2, voc)),
-            dma((2, n)),
-            dma((2, 2, voc)),
+            dma((2, voc)),
+            dma((2, voc)),
             dma((2, chunks)),
             dma((2, chunks)),
             dma((2, chunks, n // 4)),
@@ -593,15 +579,15 @@
             collective_id=0, has_side_effects=True, vmem_limit_bytes=24 * 1024 * 1024
         ),
         name="merger",
-    )(theirs, ours, in_hbm(w2), text, selector, image_pick, text_pick)
+    )(sums, in_hbm(w2), text, selector, image_pick, text_pick)
 
 
 def on_device(token_ids, routes, splice_start, vision, ln_gain, table, w_fc1, w_fc2):
-    local_ids, pick, selector, image_pick, text_pick, x = exchange(
-        token_ids, routes, splice_start, vision, ln_gain, table.shape[0], w_fc1.shape[0]
+    local_ids, pick, selector, image_pick, text_pick, x, w1 = exchange(
+        token_ids, routes, splice_start, vision, ln_gain, table.shape[0], w_fc1
     )
-    text, theirs, ours = gather_rows(local_ids, pick, x, table, w_fc1)
-    return mega(theirs, ours, w_fc2, text, selector, image_pick, text_pick)
+    text, sums = gather_rows(local_ids, pick, x, table, w1)
+    return mega(sums, w_fc2, text, selector, image_pick, text_pick)
 
 
 def solution(mesh):

time: 74.1 us -> 71.3 us (0.962)
  Pallas kernels: 72.4 us -> 69.4 us
    pallas_call x1, Pallas kernels: 52.7 us -> 48.6 us  [mega(): pl.pallas_call(mega_kernel, out_shape=jax.ShapeDtypeStruct((image_pick.sh...]
    pallas_call x1, Pallas kernels: 12.6 us -> 13.5 us  [exchange(): pl.pallas_call(body, out_shape=(shape((n, id_cap), i32), shape((n * id_ca...]
where the time goes in v5:
time: 71.3 us; the launch traced here: 70.9 us
  Pallas kernels  69.4 us (97%)
  local copies, waits for them, and re-layouts  0.8 us (1%)
    pallas_call x1, Pallas kernels, mega(): pl.pallas_call(mega_kernel, out_shape=jax.ShapeDtypeStruct((image_pick.sh...  48.6 us
    pallas_call x1, Pallas kernels, exchange(): pl.pallas_call(body, out_shape=(shape((n, id_cap), i32), shape((n * id_ca...  13.5 us
    pallas_call x1, Pallas kernels, gather_rows(): pl.pallas_call(gather_kernel, out_shape=(shape((groups * cap, width), tab...  7.31 us

profile of v5, /device:TPU:0, one launch (start us, length us, event | category | flops | bytes accessed | tf_op | source)
XLA Modules:
  0.0 70.9 jit_solution(16114259901762705425)
XLA Ops:
  0.7 13.5 %exchange.1 = (s32[8,32]{1,0:T(8,128)S(1)}, bf16[256,256]{1,0:T(8,128)(2,1)S(1)}, bf16[64,32]{1,0:T(8,128)(2,1)S(1)}, bf16[128,64]{1,0:T(8,128)(2,1)S(1)}, bf16[...) custom-call(s32[1,128]{1,0:T(1,128)} %bitcast.4, s32[1,32]{1,0:T(1,128)} %bitcast.5, ...), custom_call_target="tpu_custom_call" | custom-call | tf_op jit(solution)/shard_map/exchange/pallas_call | solution.py:201
  14.1 7.3 %gather_rows.1 = (bf16[256,2048]{1,0:T(8,128)(2,1)S(1)}, bf16[4,32,1280]{2,1,0:T(8,128)(2,1)S(1)}) custom-call(s32[8,32]{1,0:T(8,128)S(1)} %get-tuple-element.14.ids_ref, bf16[256,256]{1,0:T(8,128)(2,1)S(1)} %get-tuple-element.15.pick_ref, bf16[4,32,1280]{2,1,0:T(8,128)(2,1)S(1)} %get-tuple-element.16.x_ref, bf16[9504,2048]{1,0:T(8,128)(2,1)} %table_ref.1, ...), custom_call_target="tpu_custom_call" | custom-call | tf_op jit(solution)/shard_map/gather_rows/pallas_call | solution.py:290
  21.5 48.6 %merger.1 = bf16[128,2048]{1,0:T(8,128)(2,1)S(1)} custom-call(bf16[4,32,1280]{2,1,0:T(8,128)(2,1)S(1)} %get-tuple-element.18.sum_ref, bf16[640,2048]{1,0:T(8,128)(2,1)} %w2_hbm.1, bf16[8,32,2048]{2,1,0:T(8,128)(2,1)S(1)} %bitcast.3, bf16[64,32]{1,0:T(8,128)(2,1)S(1)} %get-tuple-element.20.selector_ref, bf16[128,64]{1,0:T(8,128)(2,1)S(1)} %get-tuple-element.21.image_ref, ...), custom_call_target="tpu_custom_call" | custom-call | tf_op jit(solution)/shard_map/merger/pallas_call | solution.py:544
  70.1 0.8 %copy.11 = bf16[128,2048]{1,0:T(8,128)(2,1)} copy(bf16[128,2048]{1,0:T(8,128)(2,1)S(1)} %merger.1) | data formatting | bytes 1048576

commit v6 on v5

--- a/solution.py
+++ b/solution.py
@@ -364,7 +364,7 @@
         for reach in range(chips - 1, -1, -1):
             for seq in range(n):
                 for other in {seq // 2 - reach, seq // 2 + reach}:
-                    if 0 <= other < chips and text_turn(other, seq // 2, chips) == turn:
+                    if 0 <= other < chips and text_turn(other, seq // 2, seq % 2, chips) == turn:
 
                         @pl.when((z == other) & (s != seq))
                         def _():
@@ -514,19 +514,20 @@
             cross_copy(column).wait_send()
 
 
-TURNS = (0, 0, 2, 2, 3, 2)
-
-
-def text_turn(source, target, chips):
+TURNS = ((0, 0, 2, 2, 3, 2), (0, 2, 2, 2, 2, 2))
+
+
+def text_turn(source, target, core, chips):
+    turns = TURNS[core]
     reach = abs(source - target)
     outer = source in (0, chips - 1)
     if reach == 0:
-        return TURNS[5]
+        return turns[5]
     if reach > chips // 2:
-        return TURNS[0]
+        return turns[0]
     if reach > chips // 4:
-        return TURNS[1] if outer else TURNS[2]
-    return TURNS[3] if outer or target in (0, chips - 1) else TURNS[4]
+        return turns[1] if outer else turns[2]
+    return turns[3] if outer or target in (0, chips - 1) else turns[4]
 
 
 def mega(sums, w2, text, selector, image_pick, text_pick):

time: 71.3 us -> 71.4 us (level)
  Pallas kernels: 69.4 us -> 70.2 us
    pallas_call x1, Pallas kernels: 48.6 us -> 49.9 us  [mega(): pl.pallas_call(mega_kernel, out_shape=jax.ShapeDtypeStruct((image_pick.sh...]
where the time goes in v6:
time: 71.4 us; the launch traced here: 71.7 us
  Pallas kernels  70.2 us (98%)
  local copies, waits for them, and re-layouts  0.8 us (1%)
    pallas_call x1, Pallas kernels, mega(): pl.pallas_call(mega_kernel, out_shape=jax.ShapeDtypeStruct((image_pick.sh...  49.9 us
    pallas_call x1, Pallas kernels, exchange(): pl.pallas_call(body, out_shape=(shape((n, id_cap), i32), shape((n * id_ca...  13.5 us
    pallas_call x1, Pallas kernels, gather_rows(): pl.pallas_call(gather_kernel, out_shape=(shape((groups * cap, width), tab...  6.8 us

profile of v6, /device:TPU:0, one launch (start us, length us, event | category | flops | bytes accessed | tf_op | source)
XLA Modules:
  0.0 71.7 jit_solution(1960530830546759927)
XLA Ops:
  0.7 13.5 %exchange.1 = (s32[8,32]{1,0:T(8,128)S(1)}, bf16[256,256]{1,0:T(8,128)(2,1)S(1)}, bf16[64,32]{1,0:T(8,128)(2,1)S(1)}, bf16[128,64]{1,0:T(8,128)(2,1)S(1)}, bf16[...) custom-call(s32[1,128]{1,0:T(1,128)} %bitcast.4, s32[1,32]{1,0:T(1,128)} %bitcast.5, ...), custom_call_target="tpu_custom_call" | custom-call | tf_op jit(solution)/shard_map/exchange/pallas_call | solution.py:201
  14.1 6.8 %gather_rows.1 = (bf16[256,2048]{1,0:T(8,128)(2,1)S(1)}, bf16[4,32,1280]{2,1,0:T(8,128)(2,1)S(1)}) custom-call(s32[8,32]{1,0:T(8,128)S(1)} %get-tuple-element.14.ids_ref, bf16[256,256]{1,0:T(8,128)(2,1)S(1)} %get-tuple-element.15.pick_ref, bf16[4,32,1280]{2,1,0:T(8,128)(2,1)S(1)} %get-tuple-element.16.x_ref, bf16[9504,2048]{1,0:T(8,128)(2,1)} %table_ref.1, ...), custom_call_target="tpu_custom_call" | custom-call | tf_op jit(solution)/shard_map/gather_rows/pallas_call | solution.py:290
  20.9 49.9 %merger.1 = bf16[128,2048]{1,0:T(8,128)(2,1)S(1)} custom-call(bf16[4,32,1280]{2,1,0:T(8,128)(2,1)S(1)} %get-tuple-element.18.sum_ref, bf16[640,2048]{1,0:T(8,128)(2,1)} %w2_hbm.1, bf16[8,32,2048]{2,1,0:T(8,128)(2,1)S(1)} %bitcast.3, bf16[64,32]{1,0:T(8,128)(2,1)S(1)} %get-tuple-element.20.selector_ref, bf16[128,64]{1,0:T(8,128)(2,1)S(1)} %get-tuple-element.21.image_ref, ...), custom_call_target="tpu_custom_call" | custom-call | tf_op jit(solution)/shard_map/merger/pallas_call | solution.py:545
  70.9 0.8 %copy.11 = bf16[128,2048]{1,0:T(8,128)(2,1)} copy(bf16[128,2048]{1,0:T(8,128)(2,1)S(1)} %merger.1) | data formatting | bytes 1048576
